TPU v7x, 128 devices: a whole 4x4x4 slice. The times are simulated.
128 devices in a mesh: tm: 64 (over y, x, z), batch: 2 (over core).
Axes of the slice: x: 4, y: 4, z: 4, core: 2. Of those that a mesh axis runs over, the one named last changes fastest.
Arguments:
- state_map: float32 [2048, 256, 256], P(('batch', 'tm')), parts along dimension 0, may hold values from -0.375 to 0.375
- input_map: float32 [2048, 64, 256], P(('batch', 'tm')), parts along dimension 0, may hold values from -0.375 to 0.375
- closed_loop: float32 [2048, 256, 256], P(('batch', 'tm')), parts along dimension 0, may hold values from -1.001 to 1.001
- feedback: float32 [2048, 64, 256], P(('batch', 'tm')), parts along dimension 0, may hold values from -0.375 to 0.375
- value_matrix: float32 [2048, 256, 256], P(('batch', 'tm')), parts along dimension 0, may hold values from -0.046875 to 1.5, as said below
- gain_inverse: float32 [2048, 64, 64], P(('batch', 'tm')), parts along dimension 0, may hold values from -0.0105 to 0.2, as said below
- input_weight: float32 [128, 64], P('batch'), parts along dimension 0, may hold values from -0.36 to 6, as said below
- state_weight: float32 [2048, 256], P(('batch', 'tm')), parts along dimension 0, may hold values from 0.1 to 3
- state_linear: float32 [2048, 256], P(('batch', 'tm')), parts along dimension 0, may hold values from -0.18 to 0.18
- input_linear: float32 [2048, 64], P(('batch', 'tm')), parts along dimension 0, may hold values from -0.18 to 0.18
- offset: float32 [2048, 256], P(('batch', 'tm')), parts along dimension 0, may hold values from -0.18 to 0.18
- upper_bound: float32 [2048, 64], P(('batch', 'tm')), parts along dimension 0, may hold values from 0.1 to 0.3
- states: float32 [2048, 256], P(('batch', 'tm')), parts along dimension 0, may hold values from -0.18 to 0.18
- inputs: float32 [2048, 64], P(('batch', 'tm')), parts along dimension 0, may hold values from -0.18 to 0.18
- multipliers: float32 [2048, 256], P(('batch', 'tm')), parts along dimension 0, may hold values from -0.18 to 0.18
- bound_mult: float32 [2048, 64], P(('batch', 'tm')), parts along dimension 0, may hold values from 0 to 0.06
- active: int32 [2048, 64], P(('batch', 'tm')), parts along dimension 0, may hold values 0 or 1
Outputs:
- state_step: float32 [2048, 256], P(('batch', 'tm')), parts along dimension 0
- input_step: float32 [2048, 64], P(('batch', 'tm')), parts along dimension 0
- multiplier_step: float32 [2048, 256], P(('batch', 'tm')), parts along dimension 0
- bound_step: float32 [2048, 64], P(('batch', 'tm')), parts along dimension 0
- kkt_norms: float32 [6], P('batch'), parts along dimension 0
There are 2 independent parts, one for each index of `batch`. A program takes and returns all parts, laid end to end along the dimension named above; each array names one. Nothing has to cross between parts.
Inputs may be any that keep to these rules, and one draw needn't show every extreme that they name: `value_matrix`: each section's matrix is symmetric. `gain_inverse`: each section's matrix is symmetric. `input_weight`: symmetric.
All inputs are finite; a program needn't handle non-finite values. No bound on the sum of `active` on one device may be relied on, other than what follows from the above.
Results may differ from a plain program's by a relative error of at most 0.0003.
Values sent between devices are 32-bit elements; how exact they have to be, the bound alone decides.
A program may use at most 128 MiB of HBM per device.

v0:
```python
import jax
import jax.numpy as jnp
from jax import lax
from jax.sharding import Mesh
from jax.sharding import PartitionSpec as P

TM = ("tm_0", "tm_1", "tm_2")
BATCH_TM = ("batch", "tm_0", "tm_1", "tm_2")


PRECISE = lax.Precision.HIGHEST
floor_share = 0.001


def shifted(x, axis, by):
    peers = lax.axis_size(axis)
    pairs = [(i, i + by) for i in range(peers) if 0 <= i + by < peers]
    return lax.ppermute(x, axis, pairs)


def neutral_like(x, identity):
    return jax.tree.map(
        lambda a, e: jnp.broadcast_to(jnp.asarray(e, a.dtype), a.shape), x, identity
    )


def prefix_by_axis(x, axes, combine, identity, reverse):
    before = start = neutral_like(x, identity)
    subtotal = x
    for axis in reversed(axes):
        peers, place = (lax.axis_size(axis), lax.axis_index(axis))
        pieces = jax.tree.map(lambda part: lax.all_gather(part, axis), subtotal)
        inside, subtotal = (start, start)
        for k in reversed(range(peers)) if reverse else range(peers):
            passed = k > place if reverse else k < place
            subtotal = combine(subtotal, jax.tree.map(lambda part: part[k], pieces))
            inside = jax.tree.map(lambda new, old: jnp.where(passed, new, old), subtotal, inside)
        before = combine(inside, before)
    return before


def copy_for_each(x, axis):
    peers = lax.axis_size(axis)
    return lax.all_to_all(jnp.broadcast_to(x[None], (peers, *x.shape)), axis, 0, 0, tiled=True)


def taken_together(x, axis):
    return copy_for_each(x, axis).sum(axis=0)


def apply_each(matrices, vectors):
    return jnp.einsum("kij,kj->ki", matrices, vectors, precision=PRECISE)


def apply_transposed(matrices, vectors):
    return jnp.einsum("kji,kj->ki", matrices, vectors, precision=PRECISE)


def compose_block(loop_mats, sources):
    dimension = loop_mats.shape[-1]

    def compose_section(carried, section_item):
        product, costate = carried
        matrix, source = section_item
        return (
            (
                jnp.dot(product, matrix, precision=PRECISE),
                jnp.dot(costate, matrix, precision=PRECISE) + source,
            ),
            None,
        )

    start = (jnp.eye(dimension, dtype=jnp.float32), jnp.zeros((dimension,), jnp.float32))
    (product, costate), unused = lax.scan(
        compose_section, start, (loop_mats, sources), reverse=True
    )
    return (product, costate)


def backward_sweep(loop_mats, sources, incoming):

    def backward_section(costate, section_item):
        matrix, source = section_item
        earlier = jnp.dot(costate, matrix, precision=PRECISE) + source
        return (earlier, (costate, earlier))

    final_state, (after, before) = lax.scan(
        backward_section, incoming, (loop_mats, sources), reverse=True
    )
    return (after, before, final_state)


def forward_sweep(loop_mats, defects, pushes, entering):

    def forward_section(carried, section_item):
        matrix, defect, pushed = section_item
        correction = carried - defect
        return (jnp.dot(matrix, correction, precision=PRECISE) + pushed, correction)

    final_state, steps = lax.scan(forward_section, entering, (loop_mats, defects, pushes))
    return (steps, final_state)


def backward_join(earlier, latter):
    return (
        jnp.dot(earlier[0], latter[0], precision=PRECISE),
        jnp.dot(earlier[1], latter[0], precision=PRECISE) + latter[1],
    )


def forward_join(earlier, latter):
    return (
        jnp.dot(latter[0], earlier[0], precision=PRECISE),
        jnp.dot(latter[0], earlier[1], precision=PRECISE) + latter[1],
    )


def make_statistics(
    defect, grad_state, grad_input, slack_gap, offset, state_linear, input_linear, bound_mult
):
    return jnp.stack(
        [
            jnp.sum(defect * defect),
            jnp.sum(grad_state * grad_state) + jnp.sum(grad_input * grad_input),
            jnp.sum(slack_gap * slack_gap),
            jnp.sum(offset * offset),
            jnp.sum(state_linear * state_linear) + jnp.sum(input_linear * input_linear),
            jnp.sum(bound_mult * bound_mult),
        ]
    )


def make_norms(totals, horizon, state_count, input_count):
    primal = totals[0] / (totals[3] + floor_share * horizon * state_count)
    dual = totals[1] / (totals[4] + floor_share * horizon * (state_count + input_count))
    complement = totals[2] / (totals[5] + floor_share * horizon * input_count)
    return jnp.sqrt(jnp.stack([primal, dual, complement]))


def local(
    state_map,
    input_map,
    closed_loop,
    feedback,
    value_matrix,
    gain_inverse,
    input_weight,
    state_weight,
    state_linear,
    input_linear,
    offset,
    upper_bound,
    states,
    inputs,
    multipliers,
    bound_mult,
    active,
):
    state_count = states.shape[1]
    input_count = inputs.shape[1]
    devices = lax.axis_size(TM)
    horizon = states.shape[0] * devices
    predicted = apply_each(state_map, states) + apply_transposed(input_map, inputs)
    from_before = shifted(predicted[-1], TM, 1)
    previous = jnp.concatenate([from_before[None], predicted[:-1]], axis=0)
    defect = states - previous - offset
    from_after = shifted(multipliers[0], TM, -1)
    following = jnp.concatenate([multipliers[1:], from_after[None]], axis=0)
    grad_state = (
        state_weight * states + state_linear + multipliers - apply_transposed(state_map, following)
    )
    grad_input = (
        jnp.einsum("ij,kj->ki", input_weight, inputs, precision=PRECISE)
        + input_linear
        - apply_each(input_map, following)
        + bound_mult
    )
    slack_gap = bound_mult * (upper_bound - inputs)
    sources = apply_each(value_matrix, defect) + grad_state + apply_transposed(feedback, grad_input)
    statistics = make_statistics(
        defect, grad_state, grad_input, slack_gap, offset, state_linear, input_linear, bound_mult
    )
    product, local_costate = compose_block(closed_loop, sources)
    identity = jnp.eye(state_count, dtype=jnp.float32)
    empty_vector = jnp.zeros((state_count,), jnp.float32)
    incoming_map, incoming = prefix_by_axis(
        (product, local_costate), TM, backward_join, (identity, empty_vector), True
    )
    after, before, unused = backward_sweep(closed_loop, sources, incoming)
    pulled = apply_each(input_map, after)
    forward_gain = -apply_each(gain_inverse, grad_input + pulled)
    pushes = apply_transposed(input_map, forward_gain)
    unused_steps, local_state = forward_sweep(closed_loop, defect, pushes, empty_vector)
    entering_map, entering = prefix_by_axis(
        (product, local_state), TM, forward_join, (identity, empty_vector), False
    )
    totals = taken_together(statistics, TM)
    state_step, final_state = forward_sweep(closed_loop, defect, pushes, entering)
    chosen = active.astype(jnp.float32)
    input_step = (1.0 - chosen) * (apply_each(feedback, state_step) + forward_gain) + chosen * (
        upper_bound - inputs
    )
    multiplier_step = apply_each(value_matrix, state_step - defect) + before
    bound_step = chosen * (
        grad_input + jnp.einsum("ij,kj->ki", input_weight, input_step, precision=PRECISE) + pulled
    )
    kkt_norms = make_norms(totals, horizon, state_count, input_count)
    return (state_step, input_step, multiplier_step, bound_step, kkt_norms)


def solution(mesh):
    split = Mesh(
        mesh.devices.reshape(4, 4, 4, mesh.shape["batch"]), ("tm_0", "tm_1", "tm_2", "batch")
    )
    return jax.shard_map(
        local,
        mesh=split,
        in_specs=(
            P(BATCH_TM, None, None),
            P(BATCH_TM, None, None),
            P(BATCH_TM, None, None),
            P(BATCH_TM, None, None),
            P(BATCH_TM, None, None),
            P(BATCH_TM, None, None),
            P("batch", None),
            P(BATCH_TM, None),
            P(BATCH_TM, None),
            P(BATCH_TM, None),
            P(BATCH_TM, None),
            P(BATCH_TM, None),
            P(BATCH_TM, None),
            P(BATCH_TM, None),
            P(BATCH_TM, None),
            P(BATCH_TM, None),
            P(BATCH_TM, None),
        ),
        out_specs=(
            P(BATCH_TM, None),
            P(BATCH_TM, None),
            P(BATCH_TM, None),
            P(BATCH_TM, None),
            P("batch"),
        ),
        check_vma=False,
    )
```

profile of v0, /device:TPU:24, one launch (start us, length us, event | category | flops | bytes accessed | tf_op | source)
XLA Modules:
  0.0 347.3 jit_solution(11131336744952943273)
XLA Ops:
  7.2 5.8 %fusion.151 = f32[16,1,256]{2,1,0:T(1,128)S(1)} fusion(f32[16,256,256]{2,1,0:T(8,128)} %param.25, f32[16,256,1]{1,0,2:T(8,128)} %bitcast.322), kind=kOutput, calls=%fused_computation.171 | convolution fusion | flops 12582912 | bytes 4227072 | tf_op jit(solution)/shard_map/kij,kj->ki/dot_general | solution.py:52
  13.8 3.8 %collective-permute-start = (f32[256]{0:T(256)S(1)}, f32[256]{0:T(256)S(1)}, u32[]{:S(2)}, u32[]{:S(2)}) collective-permute-start(f32[256]{0:T(256)S(1)} %bitcast.413), channel_id=1, source_target_pairs={{0,2},{2,4},{4,6},{6,8},{8,10},{10,12},{12,14},{14,16},{16,18},{18... | collective-permute-start | bytes 3080 | tf_op jit(solution)/shard_map/ppermute | solution.py:18
  17.7 6.4 %collective-permute-start.1 = (f32[256]{0:T(256)S(1)}, f32[256]{0:T(256)S(1)}, u32[]{:S(2)}, u32[]{:S(2)}) collective-permute-start(f32[256]{0:T(256)S(1)} %bitcast.414), channel_id=1, source_target_pairs={{2,0},{4,2},{6,4},{8,6},{10,8},{12,10},{14,12},{16,14},{18,16},{20... | collective-permute-start | bytes 3080 | tf_op jit(solution)/shard_map/ppermute | solution.py:18
  25.5 4.5 %fusion.155 = f32[16,1,256]{2,1,0:T(1,128)S(1)} fusion(f32[16,256,256]{2,1,0:T(8,128)} %param.25, f32[16,256,1]{1,0,2:T(8,128)S(1)} %maximum_bitcast_fusion), kind=kOutput, calls=%fused_computation.180 | convolution fusion | flops 12582912 | bytes 4227072 | tf_op jit(solution)/shard_map/kji,kj->ki/dot_general | solution.py:56
  31.6 3.5 %fusion.149 = f32[16,1,256]{2,1,0:T(1,128)S(1)} fusion(f32[16,256,256]{2,1,0:T(8,128)S(1)} %copy-done.2, f32[16,256,1]{1,0,2:T(8,128)S(1)} %bitcast.301), kind=kOutput, calls=%fused_computation.169 | convolution fusion | flops 12582912 | bytes 4227072 | tf_op jit(solution)/shard_map/kij,kj->ki/dot_general | solution.py:52
  35.9 45.5 %while.60 = (s32[]{:T(128)}, f32[256,256]{0,1:T(8,128)S(1)}, f32[256]{0:T(256)S(1)}, f32[16,256,256]{2,1,0:T(8,128)}, f32[16,256]{1,0:T(8,128)S(1)}, /*index=5*/s32[]{:T(128)}, s32[]{:T(128)}, s32[]{:T(128)}) while((s32[]{:T(128)}, f32[256,256]{0,1:T(8,128)S(1)}, f32[256]{0:T(256)S(1)}, f32[16,256,256]{2,1,0:T(8,128)}, ...), condition=%wide.region_1.0_spmd.clone, body=%wide.region_0.0_spmd.clone.sunk | while | flops 202113536 | bytes 1582199 | solution.py:74
  37.2 1.6 convolution_bitcast_fusion.2
  42.9 1.6 convolution_bitcast_fusion.2
  48.6 1.6 convolution_bitcast_fusion.2
  51.4 1.6 convolution_bitcast_fusion.2
  84.2 9.2 %all-gather.11 = f32[4,1,256]{2,1,0:T(1,128)S(1)} all-gather(f32[1,1,256]{2,1,0:T(1,128)S(1)} %bitcast.326), channel_id=7, replica_groups=mesh['tm_0'=4,'tm_1'=4,'tm_2'=4,'batch'=2] {'tm_2'}, dimensions={0}, use_global_device_ids=true | all-gather | bytes 5120 | tf_op jit(solution)/shard_map/all_gather | solution.py:32
  93.4 15.1 %all-gather.23.cloned.1.call-done = f32[1024,256]{0,1:T(8,128)} async-done(((f32[256,256]{0,1:T(8,128)}), f32[1024,256]{0,1:T(8,128)}) %all-gather.23.cloned.1.call-update) | async-done | bytes 1048592 | tf_op jit(solution)/shard_map/all_gather | solution.py:32
  113.7 9.7 %all-gather.12 = f32[4,1,256]{2,1,0:T(1,128)S(1)} all-gather(f32[1,1,256]{2,1,0:T(1,128)S(1)} %bitcast.383), channel_id=8, replica_groups=mesh['tm_0'=4,'tm_1'=4,'tm_2'=4,'batch'=2] {'tm_1'}, dimensions={0}, use_global_device_ids=true | all-gather | bytes 5120 | tf_op jit(solution)/shard_map/all_gather | solution.py:32
  127.4 2.1 fusion.96
  136.3 15.5 %all-gather.29.cloned.1.call-done = f32[1024,256]{1,0:T(8,128)} async-done(((f32[256,256]{1,0:T(8,128)}), f32[1024,256]{1,0:T(8,128)}) %all-gather.29.cloned.1.call-update) | async-done | bytes 1048592 | tf_op jit(solution)/shard_map/all_gather | solution.py:32
  156.5 6.7 %all-gather.13 = f32[4,1,256]{2,1,0:T(1,128)S(1)} all-gather(f32[1,1,256]{2,1,0:T(1,128)S(1)} %bitcast.384), channel_id=9, replica_groups=mesh['tm_0'=4,'tm_1'=4,'tm_2'=4,'batch'=2] {'tm_0'}, dimensions={0}, use_global_device_ids=true | all-gather | bytes 5120 | tf_op jit(solution)/shard_map/all_gather | solution.py:32
  167.8 2.1 fusion.66
  170.5 7.4 %all-gather.25.cloned.1.call-done = f32[1024,256]{1,0:T(8,128)} async-done(((f32[256,256]{1,0:T(8,128)}), f32[1024,256]{1,0:T(8,128)}) %all-gather.25.cloned.1.call-update) | async-done | bytes 1048592 | tf_op jit(solution)/shard_map/all_gather | solution.py:32
  183.9 2.0 fusion.92
  185.9 2.2 fusion.36
  188.2 2.1 fusion.31
  191.2 11.5 %all-gather.31.cloned.1.call-done = f32[1024,256]{1,0:T(8,128)} async-done(((f32[256,256]{1,0:T(8,128)}), f32[1024,256]{1,0:T(8,128)}) %all-gather.31.cloned.1.call-update) | async-done | bytes 1048592 | tf_op jit(solution)/shard_map/all_gather | solution.py:32
  208.7 21.2 %while.58 = (s32[]{:T(128)}, f32[256]{0:T(256)S(1)}, f32[16,256]{1,0:T(8,128)S(1)}, f32[16,256]{1,0:T(8,128)S(1)}, f32[16,256,256]{2,1,0:T(8,128)}, /*index=5*/f...) while((s32[]{:T(128)}, f32[256]{0:T(256)S(1)}, f32[16,256]{1,0:T(8,128)S(1)}, f32[16,256]{1,0:T(8,128)S(1)}, ...), condition=%wide.region_3.0_spmd, body=%wide.region_2.0_spmd.sunk | while | flops 786691 | bytes 273529 | solution.py:87
  231.5 2.0 fusion.181
  234.1 21.1 %while.61 = (s32[]{:T(128)}, f32[256]{0:T(256)S(1)}, f32[16,256,256]{2,1,0:T(8,128)}, f32[16,256]{1,0:T(8,128)S(1)}, f32[16,256]{1,0:T(8,128)S(1)}, /*index=5*/s32[]{:T(128)}, s32[]{:T(128)}) while((s32[]{:T(128)}, f32[256]{0:T(256)S(1)}, f32[16,256,256]{2,1,0:T(8,128)}, f32[16,256]{1,0:T(8,128)S(1)}, f32[16,256]{1,0:T(8,128)S(1)}, ...), condition=%wide.region_5.0_spmd.clone, body=%wide.region_4.0_spmd.clone.sunk | while | flops 787203 | bytes 275035 | solution.py:100
  255.2 9.9 %all-gather.14 = f32[4,1,256]{2,1,0:T(1,128)S(1)} all-gather(f32[1,1,256]{2,1,0:T(1,128)S(1)} %bitcast.325), channel_id=10, replica_groups=mesh['tm_0'=4,'tm_1'=4,'tm_2'=4,'batch'=2] {'tm_2'}, dimensions={0}, use_global_device_ids=true | all-gather | bytes 5120 | tf_op jit(solution)/shard_map/all_gather | solution.py:32
  266.6 9.5 %all-gather.15 = f32[4,1,256]{2,1,0:T(1,128)S(1)} all-gather(f32[1,1,256]{2,1,0:T(1,128)S(1)} %bitcast.381), channel_id=11, replica_groups=mesh['tm_0'=4,'tm_1'=4,'tm_2'=4,'batch'=2] {'tm_1'}, dimensions={0}, use_global_device_ids=true | all-gather | bytes 5120 | tf_op jit(solution)/shard_map/all_gather | solution.py:32
  277.8 7.6 %all-gather.16 = f32[4,1,256]{2,1,0:T(1,128)S(1)} all-gather(f32[1,1,256]{2,1,0:T(1,128)S(1)} %bitcast.382), channel_id=12, replica_groups=mesh['tm_0'=4,'tm_1'=4,'tm_2'=4,'batch'=2] {'tm_0'}, dimensions={0}, use_global_device_ids=true | all-gather | bytes 5120 | tf_op jit(solution)/shard_map/all_gather | solution.py:32
  292.5 22.0 %while.59 = (s32[]{:T(128)}, f32[256]{0:T(256)S(1)}, f32[16,256]{1,0:T(8,128)S(1)}, f32[16,256,256]{2,1,0:T(8,128)}, f32[16,256]{1,0:T(8,128)S(1)}, /*index=5*/f32[16,256]{1,0:T(8,128)S(1)}, s32[]{:T(128)}, s32[]{:T(128)}) while((s32[]{:T(128)}, f32[256]{0:T(256)S(1)}, f32[16,256]{1,0:T(8,128)S(1)}, f32[16,256,256]{2,1,0:T(8,128)}, ...), condition=%wide.region_7.0_spmd, body=%wide.region_6.0_spmd.sunk | while | flops 786946 | bytes 277085 | solution.py:100
  318.1 2.5 stack.33
  321.2 6.9 %all-to-all-start = ((f32[64,1,6]{2,1,0:T(1,128)}), f32[64,1,6]{2,1,0:T(1,128)S(1)}, u32[]{:S(2)}, u32[]{:S(2)}) async-start(f32[64,1,6]{2,1,0:T(1,128)} %broadcast_in_dim.36), calls=%async_computation | async-start | bytes 65536 | tf_op jit(solution)/shard_map/all_to_all | solution.py:44
  328.9 5.7 %fusion.143 = f32[16,1,256]{2,1,0:T(1,128)S(1)} fusion(f32[16,256,256]{2,1,0:T(8,128)} %param.29, f32[16,256,1]{1,0,2:T(8,128)S(1)} %subtract_bitcast_fusion), kind=kOutput, calls=%fused_computation.162 | convolution fusion | flops 12582912 | bytes 4227072 | tf_op jit(solution)/shard_map/kij,kj->ki/dot_general | solution.py:52
  (494 shorter events, 161.9 us)
Async XLA Ops:
  7.2 6.0 %copy-start = (f32[16,64,256]{2,1,0:T(8,128)S(1)}, f32[16,64,256]{2,1,0:T(8,128)}, u32[]{:S(2)}) copy-start(f32[16,64,256]{2,1,0:T(8,128)} %param.26) | copy-start | bytes 3145732
  7.2 6.0 %copy-start.17 = (f32[16,64]{1,0:T(8,128)S(1)}, f32[16,64]{1,0:T(8,128)}, u32[]{:S(2)}) copy-start(f32[16,64]{1,0:T(8,128)} %param.38) | copy-start | bytes 12292
  7.2 10.5 %copy-start.18 = (f32[16,256]{1,0:T(8,128)S(1)}, f32[16,256]{1,0:T(8,128)}, u32[]{:S(2)}) copy-start(f32[16,256]{1,0:T(8,128)} %param.39) | copy-start | bytes 49156
  7.2 101.2 %all-gather.23.cloned.1.call-start = ((), (), s32[]{:S(2)}) async-start(), calls=%async_computation.1 | async-start | bytes 1310720 | tf_op jit(solution)/shard_map/all_gather | solution.py:32
  13.1 17.8 %copy-start.19 = (f32[16,256]{1,0:T(8,128)S(1)}, f32[16,256]{1,0:T(8,128)}, u32[]{:S(2)}) copy-start(f32[16,256]{1,0:T(8,128)} %param.37) | copy-start | bytes 49156
  13.1 17.8 %copy-start.24 = (f32[16,256]{1,0:T(8,128)S(1)}, f32[16,256]{1,0:T(8,128)}, u32[]{:S(2)}) copy-start(f32[16,256]{1,0:T(8,128)} %param.33) | copy-start | bytes 49156
  13.1 17.8 %copy-start.25 = (f32[16,256]{1,0:T(8,128)S(1)}, f32[16,256]{1,0:T(8,128)}, u32[]{:S(2)}) copy-start(f32[16,256]{1,0:T(8,128)} %param.32) | copy-start | bytes 49156
  13.1 17.8 %copy-start.26 = (f32[16,256]{1,0:T(8,128)S(1)}, f32[16,256]{1,0:T(8,128)}, u32[]{:S(2)}) copy-start(f32[16,256]{1,0:T(8,128)} %param.35) | copy-start | bytes 49156
  13.8 17.0 %collective-permute-start = (f32[256]{0:T(256)S(1)}, f32[256]{0:T(256)S(1)}, u32[]{:S(2)}, u32[]{:S(2)}) collective-permute-start(f32[256]{0:T(256)S(1)} %bitcast.413), channel_id=1, source_target_pairs={{0,2},{2,4},{4,6},{6,8},{8,10},{10,12},{12,14},{14,16},{16,18},{18... | collective-permute-start | bytes 3080 | tf_op jit(solution)/shard_map/ppermute | solution.py:18
  17.7 7.7 %collective-permute-start.1 = (f32[256]{0:T(256)S(1)}, f32[256]{0:T(256)S(1)}, u32[]{:S(2)}, u32[]{:S(2)}) collective-permute-start(f32[256]{0:T(256)S(1)} %bitcast.414), channel_id=1, source_target_pairs={{2,0},{4,2},{6,4},{8,6},{10,8},{12,10},{14,12},{16,14},{18,16},{20... | collective-permute-start | bytes 3080 | tf_op jit(solution)/shard_map/ppermute | solution.py:18
  24.3 7.2 %copy-start.2 = (f32[16,256,256]{2,1,0:T(8,128)S(1)}, f32[16,256,256]{2,1,0:T(8,128)}, u32[]{:S(2)}) copy-start(f32[16,256,256]{2,1,0:T(8,128)} %param.29) | copy-start | bytes 12582916
  25.4 9.7 %copy-start.16 = (f32[64,64]{1,0:T(8,128)S(1)}, f32[64,64]{1,0:T(8,128)}, u32[]{:S(2)}) copy-start(f32[64,64]{1,0:T(8,128)} %param.31) | copy-start | bytes 49156
  25.4 9.7 %copy-start.20 = (f32[16,64]{1,0:T(8,128)S(1)}, f32[16,64]{1,0:T(8,128)}, u32[]{:S(2)}) copy-start(f32[16,64]{1,0:T(8,128)} %param.40) | copy-start | bytes 12292
  25.4 9.7 %copy-start.23 = (f32[16,64]{1,0:T(8,128)S(1)}, f32[16,64]{1,0:T(8,128)}, u32[]{:S(2)}) copy-start(f32[16,64]{1,0:T(8,128)} %param.34) | copy-start | bytes 12292
  25.4 9.9 %copy-start.5 = (f32[16,64,256]{2,1,0:T(8,128)S(1)}, f32[16,64,256]{2,1,0:T(8,128)}, u32[]{:S(2)}) copy-start(f32[16,64,256]{2,1,0:T(8,128)} %param.28) | copy-start | bytes 3145732
  82.1 69.6 %all-gather.29.cloned.1.call-start = ((), (), s32[]{:S(2)}) async-start(), calls=%async_computation.4 | async-start | bytes 1310720 | tf_op jit(solution)/shard_map/all_gather | solution.py:32
  108.5 21.2 %copy-start.1 = (f32[1024,256]{0,1:T(8,128)S(1)}, f32[1024,256]{0,1:T(8,128)}, u32[]{:S(2)}) copy-start(f32[1024,256]{0,1:T(8,128)} %all-gather.23.cloned.1.call-done) | copy-start | bytes 3145732
  129.4 48.4 %all-gather.25.cloned.1.call-start = ((), (), s32[]{:S(2)}) async-start(), calls=%async_computation.2 | async-start | bytes 1310720 | tf_op jit(solution)/shard_map/all_gather | solution.py:32
  130.1 0.7 copy-start.7
  134.3 36.0 %copy-start.12 = (f32[256,256]{1,0:T(8,128)S(1)}, f32[256,256]{1,0:T(8,128)}, u32[]{:S(2)}) copy-start(f32[256,256]{1,0:T(8,128)} %fusion.41) | copy-start | bytes 786436
  134.3 68.3 %all-gather.31.cloned.1.call-start = ((), (), s32[]{:S(2)}) async-start(), calls=%async_computation.5 | async-start | bytes 1310720 | tf_op jit(solution)/shard_map/all_gather | solution.py:32
  164.5 0.7 copy-start.13
  167.8 2.7 copy-start.8
  170.0 116.0 %all-gather.27.cloned.1.call-start = ((), (), s32[]{:S(2)}) async-start(), calls=%async_computation.3 | async-start | bytes 1310720 | tf_op jit(solution)/shard_map/all_gather | solution.py:32
  177.9 12.4 %copy-start.4 = (f32[1024,256]{1,0:T(8,128)S(1)}, f32[1024,256]{1,0:T(8,128)}, u32[]{:S(2)}) copy-start(f32[1024,256]{1,0:T(8,128)} %all-gather.25.cloned.1.call-done) | copy-start | bytes 3145732
  183.2 0.7 copy-start.10
  206.2 79.5 %copy-start.11 = (f32[256,256]{1,0:T(8,128)S(1)}, f32[256,256]{1,0:T(8,128)}, u32[]{:S(2)}) copy-start(f32[256,256]{1,0:T(8,128)} %fusion.26) | copy-start | bytes 786436
  233.4 83.3 %copy-start.21 = (s32[16,64]{1,0:T(8,128)S(1)}, s32[16,64]{1,0:T(8,128)}, u32[]{:S(2)}) copy-start(s32[16,64]{1,0:T(8,128)} %param.41) | copy-start | bytes 12292
  266.5 48.0 %copy-start.6 = (f32[16,64,256]{2,1,0:T(8,128)S(1)}, f32[16,64,256]{2,1,0:T(8,128)}, u32[]{:S(2)}) copy-start(f32[16,64,256]{2,1,0:T(8,128)} %param.28) | copy-start | bytes 3145732
  314.5 26.2 %copy-start.15 = (f32[16,256]{1,0:T(8,128)}, f32[16,256]{1,0:T(8,128)S(1)}, u32[]{:S(2)}) copy-start(f32[16,256]{1,0:T(8,128)S(1)} %get-tuple-element.286) | copy-start | bytes 49156
  318.1 22.7 %copy-start.22 = (f32[16,64]{1,0:T(8,128)}, f32[16,64]{1,0:T(8,128)S(1)}, u32[]{:S(2)}) copy-start(f32[16,64]{1,0:T(8,128)S(1)} %get-tuple-element.424) | copy-start | bytes 12292
  321.2 14.4 %all-to-all-start = ((f32[64,1,6]{2,1,0:T(1,128)}), f32[64,1,6]{2,1,0:T(1,128)S(1)}, u32[]{:S(2)}, u32[]{:S(2)}) async-start(f32[64,1,6]{2,1,0:T(1,128)} %broadcast_in_dim.36), calls=%async_computation | async-start | bytes 65536 | tf_op jit(solution)/shard_map/all_to_all | solution.py:44
  (3 other events, 2.1 us)
Sparse Core Ops, SparseCore 0:
  82.3 26.1 all-gather.22
  129.6 22.1 all-gather.28
  153.4 24.4 all-gather.24
  179.4 23.2 all-gather.30
  204.2 24.4 all-gather.26
where the time goes:
time: 353 us; the launch traced here: 347 us
  matrix products  182 us (52%)
  blocking collectives  52.7 us (15%)
  waiting for transfers between devices  51.1 us (14%)
  between operations  21.2 us (6%)
  starting transfers between devices  17.5 us (5%)
  local copies, waits for them, and re-layouts  12 us (3%)
  other arithmetic  7.05 us (2%)
  loops' own time  4.19 us (1%)
    all_gather x6, blocking collectives, prefix_by_axis(): pieces = jax.tree.map(lambda part: lax.all_gather(part, axis), subtotal)  52.7 us
    all_gather x5, waiting for transfers between devices, prefix_by_axis(): pieces = jax.tree.map(lambda part: lax.all_gather(part, axis), subtotal)  49.4 us
    dot_general x32, matrix products, forward_section(): return (jnp.dot(matrix, correction, precision=PRECISE) + pushed, correction)  39.2 us
    dot_general x16, matrix products, compose_section(): jnp.dot(product, matrix, precision=PRECISE)  24.8 us
    dot_general x7, matrix products, apply_each(): return jnp.einsum('kij,kj->ki', matrices, vectors, precision=PRECISE)  19.9 us
    dot_general x16, matrix products, compose_section(): jnp.dot(costate, matrix, precision=PRECISE) + source  18.7 us
    dot_general x16, matrix products, backward_section(): earlier = jnp.dot(costate, matrix, precision=PRECISE) + source  18.7 us
    dot_general x15, matrix products, backward_join(): jnp.dot(earlier[1], latter[0], precision=PRECISE) + latter[1]  15.6 us
  transfers between devices with their start and end apart: 8, of which 6 were waited for; matrix products, arithmetic and copies ran while one was open for 27% of the time, Pallas kernels for 0%

commit v1 on v0

v1 whole, which is shorter than its diff:
```python
import jax
import jax.numpy as jnp
from jax import lax
from jax.experimental import pallas as pl
from jax.experimental.pallas import tpu as pltpu
from jax.sharding import Mesh
from jax.sharding import PartitionSpec as P

TM = ("tm_0", "tm_1", "tm_2")
BATCH_TM = ("batch", "tm_0", "tm_1", "tm_2")
MESH = pl.DeviceIdType.MESH
F32 = jnp.float32
BF16 = jnp.bfloat16
PRECISE = lax.Precision.HIGHEST
floor_share = 0.001
LINE = 4
HALF = 128


def split(a):
    high = a.astype(BF16)
    return high, (a - high.astype(F32)).astype(BF16)


def mm(a, b, ca=1, cb=0):
    dims = (((ca,), (cb,)), ((), ()))
    ah, al = split(a)
    bh, bl = split(b)
    dot = lambda x, y: lax.dot_general(x, y, dims, preferred_element_type=F32)
    return dot(ah, bh) + dot(ah, bl) + dot(al, bh)


def fold(t):
    return t[:, :HALF] + t[:, HALF:] if t.shape[1] > HALF else t


def across(t):
    return jnp.sum(jnp.transpose(t), axis=0, keepdims=True)


def row_mv(w, x):
    return across(fold(w * x))


def as_column(v):
    return jnp.transpose(jnp.broadcast_to(v, (HALF, v.shape[1])))


def col_apply(vc, w):
    n = w.shape[1]
    if n > HALF:
        vc = jnp.concatenate([vc] * (n // HALF), axis=1)
    else:
        vc = vc[:, :n]
    return jnp.sum(vc * w, axis=0, keepdims=True)


def col_mv(v, w):
    return col_apply(as_column(v), w)


def identity_matrix(n):
    i = lax.broadcasted_iota(jnp.int32, (n, n), 0)
    j = lax.broadcasted_iota(jnp.int32, (n, n), 1)
    return jnp.where(i == j, 1.0, 0.0).astype(F32)


def line_products(maps, suffix, prefix):
    n = maps.shape[1]
    upper = mm(maps[3], maps[2])
    lower = mm(maps[1], maps[0])
    suffix[1] = upper
    prefix[2] = lower
    return mm(upper, lower)


def line_rest(maps, suffix, prefix):
    eye = identity_matrix(maps.shape[1])
    suffix[3] = eye
    prefix[0] = eye
    suffix[2] = maps[3]
    prefix[1] = maps[0]
    suffix[0] = mm(suffix[1], maps[1])
    prefix[3] = mm(maps[2], prefix[2])


def kernel(
    state_map_h, input_map_h, closed_loop_h, feedback_h, value_h, gain_h, weight_h,
    state_weight_h, state_linear_h, input_linear_h, offset_h, upper_h, states_h, inputs_h,
    multipliers_h, bound_h, active_h,
    state_step, input_step, multiplier_step, bound_step, norms_out,
    sm, bm, am, fm, vm, gm, iw, state_weight, state_linear, input_linear, offset, upper,
    states, inputs, mult, bound, active,
    rst, qt, phi, mmat, wst, gwst,
    gz, gx, sz, pz, sx, px, omega, tback, tforw,
    predicted, following, defect, grad_state, grad_input, sources, after, pulled, gain, pushes,
    from_next, from_prev, cz, cx, fz, fx, vy, xy, dy, ey, sy,
    vloc_z, vloc_x, xloc_z, xloc_x, cvec,
    in_sem, a_sem, m_send, m_recv, v_send, v_recv, e_send, e_recv,
):
    count, ns = states.shape
    nu = inputs.shape[1]
    y, x, z = (lax.axis_index(a) for a in TM)
    place = (y * LINE + x) * LINE + z
    last = LINE**3 - 1

    def device_at(index):
        return {
            "tm_0": lax.div(index, LINE * LINE),
            "tm_1": lax.rem(lax.div(index, LINE), LINE),
            "tm_2": lax.rem(index, LINE),
        }

    next_device = device_at(lax.rem(place + 1, last + 1))
    prev_device = device_at(lax.rem(place + last, last + 1))
    spot = {"tm_0": y, "tm_1": x, "tm_2": z}

    def peer(axis, by):
        return {axis: lax.rem(spot[axis] + by, LINE)}

    a_copies = [pltpu.make_async_copy(closed_loop_h.at[k], am.at[k], a_sem.at[k]) for k in range(count)]
    for i in range(count // 2):
        a_copies[count - 1 - i].start()
        a_copies[i].start()
    pairs = [
        (states_h, states), (inputs_h, inputs), (multipliers_h, mult), (input_map_h, bm),
        (state_map_h, sm), (state_weight_h, state_weight), (state_linear_h, state_linear),
        (input_linear_h, input_linear), (offset_h, offset), (upper_h, upper), (bound_h, bound),
        (active_h, active), (weight_h, iw), (value_h, vm), (feedback_h, fm), (gain_h, gm),
    ]
    in_copies = [pltpu.make_async_copy(s, d, in_sem.at[n]) for n, (s, d) in enumerate(pairs)]
    for copy in in_copies:
        copy.start()

    barrier = pltpu.get_barrier_semaphore()
    for axis in TM:
        for by in range(1, LINE):
            pl.semaphore_signal(barrier, inc=1, device_id=peer(axis, by), device_id_type=MESH)
    for device in (next_device, prev_device):
        pl.semaphore_signal(barrier, inc=1, device_id=device, device_id_type=MESH)

    top = count - 1
    a_copies[top].wait()
    a_copies[0].wait()
    rst[top - 1] = am[top]
    qt[1] = jnp.transpose(am[0])

    def chain_step(i):
        rst[top - 1 - i] = mm(rst[top - i], am[top - i])
        qt[i + 1] = mm(qt[i], am[i], 1, 1)

    mid = count // 2
    for i in range(1, mid):
        a_copies[top - i].wait()
        a_copies[i].wait()
    pl.loop(1, mid)(chain_step)
    whole = mm(rst[mid - 1], qt[mid], 1, 1)
    phi[...] = whole
    gz[z] = whole

    pl.semaphore_wait(barrier, 3 * (LINE - 1) + 2)

    def remote(src, dst, send, recv, device):
        return pltpu.make_async_remote_copy(
            src_ref=src, dst_ref=dst, send_sem=send, recv_sem=recv, device_id=device, device_id_type=MESH
        )

    high, low = pl.ds(0, ns // 2), pl.ds(ns // 2, ns // 2)

    def gather_maps(stage, axis, maps):
        at = spot[axis]
        right, left = peer(axis, 1), peer(axis, LINE - 1)
        before, behind = lax.rem(at + LINE - 1, LINE), lax.rem(at + 1, LINE)
        plan = [
            (at, high, right), (at, low, left), (at, low, right), (at, high, left),
            (before, high, right), (behind, low, left),
        ]
        return [
            remote(maps.at[s, rows], maps.at[s, rows], m_send.at[stage, n], m_recv.at[stage, n], dev)
            for n, (s, rows, dev) in enumerate(plan)
        ]

    def relay(copies):
        copies[0].wait_recv()
        copies[4].start()
        copies[1].wait_recv()
        copies[5].start()

    def finish(copies):
        for copy in copies[2:]:
            copy.wait_recv()
        for copy in copies:
            copy.wait_send()

    def gather_vectors(stage, axis, buf):
        at = spot[axis]
        return [
            remote(buf.at[at], buf.at[at], v_send.at[stage, by - 1], v_recv.at[stage, by - 1], peer(axis, by))
            for by in range(1, LINE)
        ]

    def run(copies):
        for copy in copies:
            copy.start()

    def wait(copies):
        for copy in copies:
            copy.wait_recv()
        for copy in copies:
            copy.wait_send()

    z_maps = gather_maps(0, "tm_2", gz)
    run(z_maps[:4])

    for copy in in_copies[:5]:
        copy.wait()
    to_prev = remote(mult.at[pl.ds(0, 8)], from_next, e_send.at[0], e_recv.at[0], prev_device)
    to_prev.start()

    for i in range(mid, top):
        pass
    pl.loop(mid, top)(chain_step)

    def predict(k):
        at = pl.ds(k, 1)
        predicted[at, :] = row_mv(sm[k], states[at, :]) + col_mv(inputs[at, :], bm[k])

    pl.loop(0, count)(predict)
    to_next = remote(predicted.at[pl.ds(count - 8, 8)], from_prev, e_send.at[1], e_recv.at[1], next_device)
    to_next.start()
    relay(z_maps)

    to_prev.wait_recv()
    following[pl.ds(0, count - 1), :] = mult[pl.ds(1, count - 1), :]
    following[pl.ds(count - 1, 1), :] = jnp.where(place == last, 0.0, from_next[pl.ds(0, 1), :])
    for copy in in_copies[5:]:
        copy.wait()

    def gradients(k):
        at = pl.ds(k, 1)
        ahead = following[at, :]
        grad_state[at, :] = col_mv(ahead, sm[k])
        grad_input[at, :] = row_mv(bm[k], ahead)

    pl.loop(0, count)(gradients)
    grad_state[...] = state_weight[...] * states[...] + state_linear[...] + mult[...] - grad_state[...]
    weighted = lax.dot_general(
        inputs[...], iw[...], (((1,), (1,)), ((), ())), precision=PRECISE, preferred_element_type=F32
    )
    grad_input[...] = weighted + input_linear[...] - grad_input[...] + bound[...]

    to_next.wait_recv()
    defect[pl.ds(1, count - 1), :] = (
        states[pl.ds(1, count - 1), :] - predicted[pl.ds(0, count - 1), :] - offset[pl.ds(1, count - 1), :]
    )
    entered = jnp.where(place == 0, 0.0, from_prev[pl.ds(7, 1), :])
    defect[pl.ds(0, 1), :] = states[pl.ds(0, 1), :] - entered - offset[pl.ds(0, 1), :]

    def source(k):
        at = pl.ds(k, 1)
        sources[at, :] = row_mv(vm[k], defect[at, :]) + grad_state[at, :] + col_mv(grad_input[at, :], fm[k])

    pl.loop(0, count)(source)

    def gather_source(k, acc):
        return acc + fold(qt[k] * sources[pl.ds(k, 1), :])

    acc = lax.fori_loop(1, count, gather_source, jnp.zeros((ns, HALF), F32))
    local_costate = across(acc) + sources[pl.ds(0, 1), :]
    cvec[pl.ds(0, 1), :] = local_costate

    slack = bound[...] * (upper[...] - inputs[...])
    lane = lax.broadcasted_iota(jnp.int32, (1, ns), 1)
    squares = lambda t: jnp.sum(t * t)
    sums = [
        squares(defect[...]), squares(grad_state[...]) + squares(grad_input[...]), squares(slack),
        squares(offset[...]), squares(state_linear[...]) + squares(input_linear[...]), squares(bound[...]),
    ]
    stats = jnp.zeros((1, ns), F32)
    for n, s in enumerate(sums):
        stats = jnp.where(lane == n, s, stats)

    cz[z, pl.ds(0, 1), :] = local_costate
    cz[z, pl.ds(1, 1), :] = stats
    cz[z, pl.ds(2, 6), :] = jnp.zeros((6, ns), F32)
    c_line = gather_vectors(0, "tm_2", cz)
    run(c_line)

    finish(z_maps)
    group = line_products(gz, sz, pz)
    gx[x] = group
    x_maps = gather_maps(1, "tm_1", gx)
    run(x_maps[:4])

    def backward(i, v):
        k = top - i
        after[pl.ds(k, 1), :] = v
        return col_mv(v, am[k]) + sources[pl.ds(k, 1), :]

    lax.fori_loop(0, count, backward, jnp.zeros((1, ns), F32))

    def respond(k):
        at = pl.ds(k, 1)
        pull = row_mv(bm[k], after[at, :])
        pulled[at, :] = pull
        step = -row_mv(gm[k], grad_input[at, :] + pull)
        gain[at, :] = step
        pushes[at, :] = col_mv(step, bm[k])

    pl.loop(0, count)(respond)

    def gather_push(k, acc):
        return acc + fold(rst[k] * (pushes[pl.ds(k, 1), :] - defect[pl.ds(k + 1, 1), :]))

    acc = lax.fori_loop(0, top, gather_push, -fold(phi[...] * defect[pl.ds(0, 1), :]))
    f_zero = across(acc) + pushes[pl.ds(top, 1), :]

    relay(x_maps)

    def reach(k):
        w = mm(bm[k], rst[k], 1, 1)
        rows = pl.ds(pl.multiple_of(k * nu, nu), nu)
        wst[rows, :] = w
        gwst[rows, :] = mm(gm[k], w)

    pl.loop(0, top)(reach)
    wst[pl.ds(top * nu, nu), :] = bm[top]
    gwst[pl.ds(top * nu, nu), :] = mm(gm[top], bm[top])
    mmat[...] = mm(wst[...], gwst[...], 0, 0)

    line_rest(gz, sz, pz)
    wait(c_line)

    def line_backward(buf, maps, store):
        v = buf[LINE - 1, pl.ds(0, 1), :]
        store[LINE - 1] = jnp.zeros((8, ns), F32)
        for p in reversed(range(LINE - 1)):
            store[p] = jnp.broadcast_to(v, (8, ns))
            v = col_mv(v, maps[p]) + buf[p, pl.ds(0, 1), :]
        total = jnp.sum(buf[:, 1:2, :], axis=0)
        return v, total

    group_costate, totals = line_backward(cz, gz, vloc_z)
    cx[x, pl.ds(0, 1), :] = group_costate
    cx[x, pl.ds(1, 1), :] = totals
    cx[x, pl.ds(2, 6), :] = jnp.zeros((6, ns), F32)
    cx_line = gather_vectors(1, "tm_1", cx)
    run(cx_line)
    wait(cx_line)

    finish(x_maps)
    omega[...] = line_products(gx, sx, px)
    plane_costate, totals = line_backward(cx, gx, vloc_x)
    sy[y] = jnp.broadcast_to(totals, (8, ns))
    s_line = gather_vectors(4, "tm_0", sy)
    run(s_line)
    line_rest(gx, sx, px)
    tback[...] = mm(sx[x], sz[z])
    tforw[...] = mm(pz[z], px[x])
    t_zero = col_mv(vloc_x[x, pl.ds(0, 1), :], sz[z]) + vloc_z[z, pl.ds(0, 1), :]

    down = remote(dy, vy, e_send.at[2], e_recv.at[2], peer("tm_0", LINE - 1))

    @pl.when(y == LINE - 1)
    def _():
        vy[...] = jnp.zeros((8, ns), F32)

    @pl.when(y < LINE - 1)
    def _():
        down.wait_recv()

    plane_in = vy[pl.ds(0, 1), :]

    @pl.when(y > 0)
    def _():
        dy[...] = jnp.broadcast_to(col_mv(plane_in, omega[...]) + plane_costate, (8, ns))
        down.start()

    v = col_mv(plane_in, tback[...]) + t_zero
    f_own = f_zero - row_mv(mmat[...], v)
    fz[z] = jnp.broadcast_to(f_own, (8, ns))
    f_line = gather_vectors(2, "tm_2", fz)
    run(f_line)

    vc = as_column(v)

    def lift(k):
        at = pl.ds(k, 1)
        after[at, :] = after[at, :] + col_apply(vc, rst[k])

    pl.loop(0, top)(lift)
    after[pl.ds(top, 1), :] = v
    before_first = col_apply(vc, phi[...]) + cvec[pl.ds(0, 1), :]

    def line_forward(buf, suffix):
        acc = jnp.zeros((ns, HALF), F32)
        for p in range(LINE):
            acc = acc + fold(suffix[p] * buf[p, pl.ds(0, 1), :])
        return across(acc)

    def line_states(buf, maps, store):
        store[0] = jnp.zeros((8, ns), F32)
        v = buf[0, pl.ds(0, 1), :]
        store[1] = jnp.broadcast_to(v, (8, ns))
        for p in range(1, LINE - 1):
            v = row_mv(maps[p], v) + buf[p, pl.ds(0, 1), :]
            store[p + 1] = jnp.broadcast_to(v, (8, ns))

    wait(f_line)
    fx[x] = jnp.broadcast_to(line_forward(fz, sz), (8, ns))
    fx_line = gather_vectors(3, "tm_1", fx)
    run(fx_line)

    pl.loop(0, count)(respond)

    wait(fx_line)
    plane_state = line_forward(fx, sx)

    up = remote(ey, xy, e_send.at[3], e_recv.at[3], peer("tm_0", 1))

    def pass_up():
        entering = xy[pl.ds(0, 1), :]
        ey[...] = jnp.broadcast_to(row_mv(omega[...], entering) + plane_state, (8, ns))
        up.start()

    @pl.when(y == 0)
    def _():
        xy[...] = jnp.zeros((8, ns), F32)
        ey[...] = jnp.broadcast_to(plane_state, (8, ns))
        up.start()

    line_states(fz, gz, xloc_z)
    line_states(fx, gx, xloc_x)
    x_zero = row_mv(pz[z], xloc_x[x, pl.ds(0, 1), :]) + xloc_z[z, pl.ds(0, 1), :]

    def forward(k, carried):
        correction = carried - defect[pl.ds(k, 1), :]
        state_step[pl.ds(k, 1), :] = correction
        return row_mv(am[k], correction) + pushes[pl.ds(k, 1), :]

    @pl.when(y > 0)
    def _():
        up.wait_recv()

    @pl.when((y > 0) & (y < LINE - 1))
    def _():
        pass_up()

    lax.fori_loop(0, count, forward, jnp.zeros((1, ns), F32))

    x_in = row_mv(tforw[...], xy[pl.ds(0, 1), :]) + x_zero
    xc = as_column(x_in)
    state_step[pl.ds(0, 1), :] = state_step[pl.ds(0, 1), :] + x_in

    def settle(k):
        at = pl.ds(k, 1)
        state_step[at, :] = state_step[at, :] + col_apply(xc, qt[k])

    pl.loop(1, count)(settle)

    def close(k):
        at = pl.ds(k, 1)
        here = state_step[at, :]
        multiplier_step[at, :] = row_mv(vm[k], here - defect[at, :])
        input_step[at, :] = row_mv(fm[k], here)

    pl.loop(0, count)(close)
    multiplier_step[pl.ds(1, count - 1), :] = (
        multiplier_step[pl.ds(1, count - 1), :] + after[pl.ds(0, count - 1), :]
    )
    multiplier_step[pl.ds(0, 1), :] = multiplier_step[pl.ds(0, 1), :] + before_first
    chosen = active[...].astype(F32)
    step = (1.0 - chosen) * (input_step[...] + gain[...]) + chosen * (upper[...] - inputs[...])
    input_step[...] = step
    weighted = lax.dot_general(
        step, iw[...], (((1,), (1,)), ((), ())), precision=PRECISE, preferred_element_type=F32
    )
    bound_step[...] = chosen * (grad_input[...] + weighted + pulled[...])

    wait(s_line)
    totals = jnp.sum(sy[:, 0:1, :], axis=0)
    horizon = count * LINE**3
    pick = lambda n: jnp.sum(jnp.where(lane == n, totals, 0.0), axis=1, keepdims=True)
    primal = pick(0) / (pick(3) + floor_share * horizon * ns)
    dual = pick(1) / (pick(4) + floor_share * horizon * (ns + nu))
    complement = pick(2) / (pick(5) + floor_share * horizon * nu)
    lanes = lax.broadcasted_iota(jnp.int32, norms_out.shape, 1)
    values = jnp.where(lanes == 0, primal, jnp.where(lanes == 1, dual, complement))
    norms_out[...] = jnp.sqrt(values)

    to_prev.wait_send()
    to_next.wait_send()

    @pl.when(y > 0)
    def _():
        down.wait_send()

    @pl.when(y < LINE - 1)
    def _():
        up.wait_send()


def local(*args):
    states, inputs = args[12], args[13]
    count, ns = states.shape
    nu = inputs.shape[1]
    v = lambda *shape: pltpu.VMEM(shape, F32)
    dma = lambda *shape: pltpu.SemaphoreType.DMA(shape)
    scratch = [
        v(count, ns, ns), v(count, nu, ns), v(count, ns, ns), v(count, nu, ns), v(count, ns, ns),
        v(count, nu, nu), v(nu, nu), v(count, ns), v(count, ns), v(count, nu), v(count, ns), v(count, nu),
        v(count, ns), v(count, nu), v(count, ns), v(count, nu), pltpu.VMEM((count, nu), jnp.int32),
        v(count, ns, ns), v(count, ns, ns), v(ns, ns), v(ns, ns), v(count * nu, ns), v(count * nu, ns),
        v(LINE, ns, ns), v(LINE, ns, ns), v(LINE, ns, ns), v(LINE, ns, ns), v(LINE, ns, ns), v(LINE, ns, ns),
        v(ns, ns), v(ns, ns), v(ns, ns),
        v(count, ns), v(count, ns), v(count, ns), v(count, ns), v(count, nu), v(count, ns), v(count, ns),
        v(count, nu), v(count, nu), v(count, ns),
        v(8, ns), v(8, ns), v(LINE, 8, ns), v(LINE, 8, ns), v(LINE, 8, ns), v(LINE, 8, ns),
        v(8, ns), v(8, ns), v(8, ns), v(8, ns), v(LINE, 8, ns),
        v(LINE, 8, ns), v(LINE, 8, ns), v(LINE, 8, ns), v(LINE, 8, ns), v(8, ns),
        dma(16), dma(count), dma(2, 6), dma(2, 6), dma(5, LINE - 1), dma(5, LINE - 1), dma(4), dma(4),
    ]
    vmem = pl.BlockSpec(memory_space=pltpu.VMEM)
    out = pl.pallas_call(
        kernel,
        out_shape=[
            jax.ShapeDtypeStruct((count, ns), F32),
            jax.ShapeDtypeStruct((count, nu), F32),
            jax.ShapeDtypeStruct((count, ns), F32),
            jax.ShapeDtypeStruct((count, nu), F32),
            jax.ShapeDtypeStruct((8, HALF), F32),
        ],
        in_specs=[pl.BlockSpec(memory_space=pl.ANY)] * len(args),
        out_specs=[vmem] * 5,
        scratch_shapes=scratch,
        compiler_params=pltpu.CompilerParams(
            collective_id=0, has_side_effects=True, vmem_limit_bytes=60 * 1024 * 1024
        ),
        name="riccati",
    )(*args)
    return (*out[:4], out[4][0, :3])


def solution(mesh):
    lines = Mesh(
        mesh.devices.reshape(LINE, LINE, LINE, mesh.shape["batch"]), ("tm_0", "tm_1", "tm_2", "batch")
    )
    cube, flat = P(BATCH_TM, None, None), P(BATCH_TM, None)
    return jax.shard_map(
        local,
        mesh=lines,
        in_specs=(cube,) * 6 + (P("batch", None),) + (flat,) * 10,
        out_specs=(flat, flat, flat, flat, P("batch")),
        check_vma=False,
    )
```

time: 353 us -> 87.3 us (0.25); the launches traced: 347 us -> 86.8 us
  matrix products: 182 us -> 0 us
  Pallas kernels: 0 us -> 79.7 us
  blocking collectives: 52.7 us -> 0 us
  waiting for transfers between devices: 51.1 us -> 0 us
  between operations: 21.2 us -> 0.65 us
  starting transfers between devices: 17.5 us -> 0 us
  other arithmetic: 7.05 us -> 0 us
  local copies, waits for them, and re-layouts: 12 us -> 6.43 us
  loops' own time: 4.19 us -> 0 us
    dot_general x143 -> x0, matrix products: 182 us -> none  [the longest x32 39.2 us: forward_section(): return (jnp.dot(matrix, correction, precision=PRECISE) + pushed, correction)]
    pallas_call x0 -> x1, Pallas kernels: none -> 79.7 us  [local(): pl.pallas_call(kernel, out_shape=[jax.ShapeDtypeStruct((count, ns), F32),...]
    all_gather x6 -> x0, blocking collectives: 52.7 us -> none  [prefix_by_axis(): pieces = jax.tree.map(lambda part: lax.all_gather(part, axis), subtotal)]
    all_gather x5 -> x0, waiting for transfers between devices: 49.4 us -> none  [prefix_by_axis(): pieces = jax.tree.map(lambda part: lax.all_gather(part, axis), subtotal)]
    ppermute x2 -> x0, starting transfers between devices: 10.2 us -> none  [shifted(): return lax.ppermute(x, axis, pairs)]
    all_to_all x1 -> x0, starting transfers between devices: 6.88 us -> none  [copy_for_each(): lax.all_to_all(jnp.broadcast_to(x[None], (peers, *x.shape)), axis, 0, 0,...]
    another operation x4 -> x0, loops' own time: 4.19 us -> none  [the longest x2 2.56 us: forward_sweep(): lax.scan(forward_section, entering, (loop_mats, defects, pushes))]
  transfers between devices with their start and end apart: 8 -> 0, of which waited for: 6 -> 0; matrix products, arithmetic and copies ran while one was open for 27% -> 0% of each run, Pallas kernels for 0% -> 0%
where the time goes in v1:
time: 87.3 us; the launch traced here: 86.8 us
  Pallas kernels  79.7 us (91%)
  local copies, waits for them, and re-layouts  6.43 us (7%)
    pallas_call x1, Pallas kernels, local(): pl.pallas_call(kernel, out_shape=[jax.ShapeDtypeStruct((count, ns), F32),...  79.7 us
    unnamed x4, local copies, waits for them, and re-layouts  5.23 us

profile of v1, /device:TPU:24, one launch (start us, length us, event | category | flops | bytes accessed | tf_op | source)
XLA Modules:
  0.0 86.8 jit_solution(14102103538391214590)
XLA Ops:
  0.6 79.7 %riccati.1 = (f32[16,256]{1,0:T(8,128)}, f32[16,64]{1,0:T(8,128)}, f32[16,256]{1,0:T(8,128)}, f32[16,64]{1,0:T(8,128)}, f32[8,128]{1,0:T(8,128)}) custom-call(f32[16,256,256]{2,1,0:T(8,128)} %state_map_h.1, f32[16,64,256]{2,1,0:T(8,128)} %input_map_h.1, f32[16,256,256]{2,1,0:T(8,128)} %closed_loop_h.1, f32[16,64,256]{2,1,0:T(8,128)} %feedback_h.1, ...), custom_call_target="tpu_custom_call" | custom-call | tf_op jit(solution)/shard_map/riccati/pallas_call | solution.py:524
  80.4 1.2 %slice_bitcast_fusion = f32[3]{0:T(128)} fusion(f32[8,128]{1,0:T(8,128)} %get-tuple-element.14), kind=kLoop, calls=%fused_computation | loop fusion | bytes 24 | tf_op jit(solution)/shard_map/squeeze | solution.py:541
  81.6 1.3 %copy.26 = f32[16,256]{1,0:T(8,128)} copy(f32[16,256]{1,0:T(8,128)} %get-tuple-element.20) | data formatting | bytes 32768
  82.9 1.3 %copy.27 = f32[16,64]{1,0:T(8,128)} copy(f32[16,64]{1,0:T(8,128)} %get-tuple-element.21) | data formatting | bytes 8192
  84.2 1.3 %copy.28 = f32[16,256]{1,0:T(8,128)} copy(f32[16,256]{1,0:T(8,128)} %get-tuple-element.22) | data formatting | bytes 32768
  85.5 1.3 %copy.29 = f32[16,64]{1,0:T(8,128)} copy(f32[16,64]{1,0:T(8,128)} %get-tuple-element.23) | data formatting | bytes 8192

commit v2 on v1

v2 whole, which is shorter than its diff:
```python
import jax
import jax.numpy as jnp
from jax import lax
from jax.experimental import pallas as pl
from jax.experimental.pallas import tpu as pltpu
from jax.sharding import Mesh
from jax.sharding import PartitionSpec as P

TM = ("tm_0", "tm_1", "tm_2")
BATCH_TM = ("batch", "tm_0", "tm_1", "tm_2")
MESH = pl.DeviceIdType.MESH
F32 = jnp.float32
BF16 = jnp.bfloat16
PRECISE = lax.Precision.HIGHEST
floor_share = 0.001
LINE = 4
HALF = 128


def split(a):
    high = a.astype(BF16)
    return high, (a - high.astype(F32)).astype(BF16)


def mm(a, b, ca=1, cb=0):
    dims = (((ca,), (cb,)), ((), ()))
    ah, al = split(a)
    bh, bl = split(b)
    dot = lambda x, y: lax.dot_general(x, y, dims, preferred_element_type=F32)
    return dot(ah, bh) + dot(ah, bl) + dot(al, bh)


def fold(t):
    return t[:, :HALF] + t[:, HALF:] if t.shape[1] > HALF else t


def across(t):
    return jnp.sum(jnp.transpose(t), axis=0, keepdims=True)


def row_mv(w, x):
    return across(fold(w * x))


def as_column(v):
    return jnp.transpose(jnp.broadcast_to(v, (HALF, v.shape[1])))


def col_apply(vc, w):
    n = w.shape[1]
    if n > HALF:
        vc = jnp.concatenate([vc] * (n // HALF), axis=1)
    else:
        vc = vc[:, :n]
    return jnp.sum(vc * w, axis=0, keepdims=True)


def col_mv(v, w):
    return col_apply(as_column(v), w)


def identity_matrix(n):
    i = lax.broadcasted_iota(jnp.int32, (n, n), 0)
    j = lax.broadcasted_iota(jnp.int32, (n, n), 1)
    return jnp.where(i == j, 1.0, 0.0).astype(F32)


def line_products(maps, suffix, prefix):
    n = maps.shape[1]
    upper = mm(maps[3], maps[2])
    lower = mm(maps[1], maps[0])
    suffix[1] = upper
    prefix[2] = lower
    return mm(upper, lower)


def line_rest(maps, suffix, prefix):
    eye = identity_matrix(maps.shape[1])
    suffix[3] = eye
    prefix[0] = eye
    suffix[2] = maps[3]
    prefix[1] = maps[0]
    suffix[0] = mm(suffix[1], maps[1])
    prefix[3] = mm(maps[2], prefix[2])


def kernel(
    state_map_h, input_map_h, closed_loop_h, feedback_h, value_h, gain_h, weight_h,
    state_weight_h, state_linear_h, input_linear_h, offset_h, upper_h, states_h, inputs_h,
    multipliers_h, bound_h, active_h,
    packed,
    sm, bm, am, fm, vm, gm, iw, state_weight, state_linear, input_linear, offset, upper,
    states, inputs, mult, bound, active,
    rst, qt, tree, phi, mmat, wst, gwst,
    gz, gx, sz, pz, sx, px, omega, om1, om2, tback, tforw,
    predicted, following, defect, grad_state, grad_input, sources, after, pulled, gain, pushes, state_step,
    edge, from_next, from_prev, cz, cx, plane, fy, vy, dy, sy,
    vloc_z, vloc_x, cvec,
    in_sem, a_sem, m_send, m_recv, v_send, v_recv, e_send, e_recv, p_send, p_recv, y_send, y_recv, f_send, f_recv,
):
    count, ns = states.shape
    nu = inputs.shape[1]
    y, x, z = (lax.axis_index(a) for a in TM)
    place = (y * LINE + x) * LINE + z
    last = LINE**3 - 1
    top = count - 1

    def device_at(index):
        return {
            "tm_0": lax.div(index, LINE * LINE),
            "tm_1": lax.rem(lax.div(index, LINE), LINE),
            "tm_2": lax.rem(index, LINE),
        }

    next_device = device_at(lax.rem(place + 1, last + 1))
    prev_device = device_at(lax.rem(place + last, last + 1))
    spot = {"tm_0": y, "tm_1": x, "tm_2": z}

    def peer(axis, by):
        return {axis: lax.rem(spot[axis] + by, LINE)}

    offsets = [(i, j) for i in range(LINE) for j in range(LINE) if i or j]

    def in_plane(i, j):
        return {"tm_1": lax.rem(x + i, LINE), "tm_2": lax.rem(z + j, LINE)}

    a_copies = [pltpu.make_async_copy(closed_loop_h.at[k], am.at[k], a_sem.at[k]) for k in range(count)]
    pairs = [
        (states_h, states), (inputs_h, inputs), (input_map_h.at[top], bm.at[top]), (state_map_h.at[top], sm.at[top]),
        (multipliers_h, mult), (input_map_h.at[pl.ds(0, top)], bm.at[pl.ds(0, top)]),
        (state_map_h.at[pl.ds(0, top)], sm.at[pl.ds(0, top)]), (state_weight_h, state_weight),
        (state_linear_h, state_linear), (input_linear_h, input_linear), (offset_h, offset), (upper_h, upper),
        (bound_h, bound), (active_h, active), (weight_h, iw), (value_h, vm), (feedback_h, fm), (gain_h, gm),
    ]
    in_copies = [pltpu.make_async_copy(s, d, in_sem.at[n]) for n, (s, d) in enumerate(pairs)]
    for copy in in_copies[:5]:
        copy.start()
    for copy in a_copies:
        copy.start()

    barrier = pltpu.get_barrier_semaphore()
    for by in range(1, LINE):
        pl.semaphore_signal(barrier, inc=1, device_id=peer("tm_0", by), device_id_type=MESH)
    for i, j in offsets:
        pl.semaphore_signal(barrier, inc=1, device_id=in_plane(i, j), device_id_type=MESH)
    for device in (next_device, prev_device):
        pl.semaphore_signal(barrier, inc=1, device_id=device, device_id_type=MESH)

    def predict(k):
        at = pl.ds(k, 1)
        predicted[at, :] = row_mv(sm[k], states[at, :]) + col_mv(inputs[at, :], bm[k])

    for copy in a_copies[: count // 2]:
        copy.wait()
    for i in range(count // 4):
        tree[i] = mm(am[2 * i + 1], am[2 * i])
    for copy in a_copies[count // 2 :] + in_copies[:5]:
        copy.wait()
    predict(top)
    edge[...] = jnp.broadcast_to(predicted[pl.ds(top, 1), :], (8, ns))
    for copy in in_copies[5:]:
        copy.start()
    for i in range(count // 4, count // 2):
        tree[i] = mm(am[2 * i + 1], am[2 * i])
    level = [tree[i] for i in range(count // 2)]
    while len(level) > 1:
        level = [mm(level[i + 1], level[i]) for i in range(0, len(level), 2)]
    phi[...] = level[0]
    gz[z] = level[0]

    pl.semaphore_wait(barrier, (LINE - 1) + len(offsets) + 2)

    def remote(src, dst, send, recv, device):
        return pltpu.make_async_remote_copy(
            src_ref=src, dst_ref=dst, send_sem=send, recv_sem=recv, device_id=device, device_id_type=MESH
        )

    high, low = pl.ds(0, ns // 2), pl.ds(ns // 2, ns // 2)

    def gather_maps(stage, axis, maps):
        at = spot[axis]
        right, left = peer(axis, 1), peer(axis, LINE - 1)
        before, behind = lax.rem(at + LINE - 1, LINE), lax.rem(at + 1, LINE)
        plan = [
            (at, high, right), (at, low, left), (at, low, right), (at, high, left),
            (before, high, right), (behind, low, left),
        ]
        return [
            remote(maps.at[s, rows], maps.at[s, rows], m_send.at[stage, n], m_recv.at[stage, n], dev)
            for n, (s, rows, dev) in enumerate(plan)
        ]

    def relay(copies):
        copies[0].wait_recv()
        copies[4].start()
        copies[1].wait_recv()
        copies[5].start()

    def gather_vectors(stage, axis, buf):
        at = spot[axis]
        return [
            remote(buf.at[at], buf.at[at], v_send.at[stage, by - 1], v_recv.at[stage, by - 1], peer(axis, by))
            for by in range(1, LINE)
        ]

    def run(copies):
        for copy in copies:
            copy.start()

    def arrive(copies):
        for copy in copies:
            copy.wait_recv()

    to_prev = remote(mult.at[pl.ds(0, 8)], from_next, e_send.at[0], e_recv.at[0], prev_device)
    to_next = remote(edge, from_prev, e_send.at[1], e_recv.at[1], next_device)
    z_maps = gather_maps(0, "tm_2", gz)
    run([to_prev, to_next] + z_maps[:4])

    half = count // 2
    rst[top - 1] = am[top]
    rst[top - 2] = tree[half - 1]
    qt[1] = jnp.transpose(am[0])
    qt[2] = jnp.transpose(tree[0])

    def chain_step(i):
        j = half - 1 - i
        suffix, prefix = rst[2 * j + 1], qt[2 * i]
        rst[2 * j] = mm(suffix, am[2 * j + 1])
        rst[2 * j - 1] = mm(suffix, tree[j])
        qt[2 * i + 1] = mm(prefix, am[2 * i], 1, 1)
        qt[2 * i + 2] = mm(prefix, tree[i], 1, 1)

    pl.loop(1, half - 1)(chain_step)
    rst[0] = mm(rst[1], am[1])
    qt[top] = mm(qt[top - 1], am[top - 1], 1, 1)

    for copy in in_copies[5:]:
        copy.wait()
    pl.loop(0, top, unroll=5)(predict)

    relay(z_maps)

    to_prev.wait_recv()
    following[pl.ds(0, top), :] = mult[pl.ds(1, top), :]
    following[pl.ds(top, 1), :] = jnp.where(place == last, 0.0, from_next[pl.ds(0, 1), :])

    def gradients(k):
        at = pl.ds(k, 1)
        ahead = following[at, :]
        grad_state[at, :] = col_mv(ahead, sm[k])
        grad_input[at, :] = row_mv(bm[k], ahead)

    pl.loop(0, count, unroll=4)(gradients)
    grad_state[...] = state_weight[...] * states[...] + state_linear[...] + mult[...] - grad_state[...]
    weighted = lax.dot_general(
        inputs[...], iw[...], (((1,), (1,)), ((), ())), precision=PRECISE, preferred_element_type=F32
    )
    grad_input[...] = weighted + input_linear[...] - grad_input[...] + bound[...]

    to_next.wait_recv()
    defect[pl.ds(1, top), :] = states[pl.ds(1, top), :] - predicted[pl.ds(0, top), :] - offset[pl.ds(1, top), :]
    entered = jnp.where(place == 0, 0.0, from_prev[pl.ds(0, 1), :])
    defect[pl.ds(0, 1), :] = states[pl.ds(0, 1), :] - entered - offset[pl.ds(0, 1), :]

    def source(k):
        at = pl.ds(k, 1)
        sources[at, :] = row_mv(vm[k], defect[at, :]) + grad_state[at, :] + col_mv(grad_input[at, :], fm[k])

    pl.loop(0, count, unroll=4)(source)

    def gather_source(k, acc):
        return acc + fold(qt[k] * sources[pl.ds(k, 1), :])

    acc = lax.fori_loop(1, count, gather_source, jnp.zeros((ns, HALF), F32), unroll=3)
    local_costate = across(acc) + sources[pl.ds(0, 1), :]
    cvec[pl.ds(0, 1), :] = local_costate

    slack = bound[...] * (upper[...] - inputs[...])
    lane = lax.broadcasted_iota(jnp.int32, (1, ns), 1)
    squares = lambda t: jnp.sum(t * t)
    sums = [
        squares(defect[...]), squares(grad_state[...]) + squares(grad_input[...]), squares(slack),
        squares(offset[...]), squares(state_linear[...]) + squares(input_linear[...]), squares(bound[...]),
    ]
    stats = jnp.zeros((1, ns), F32)
    for n, s in enumerate(sums):
        stats = jnp.where(lane == n, s, stats)

    cz[z, pl.ds(0, 1), :] = local_costate
    cz[z, pl.ds(1, 1), :] = stats
    cz[z, pl.ds(2, 6), :] = jnp.zeros((6, ns), F32)
    c_line = gather_vectors(0, "tm_2", cz)
    run(c_line)

    arrive(z_maps[2:])
    gx[x] = line_products(gz, sz, pz)
    x_maps = gather_maps(1, "tm_1", gx)

    def line_backward(buf, maps, store):
        v = buf[LINE - 1, pl.ds(0, 1), :]
        store[LINE - 1] = jnp.zeros((8, ns), F32)
        for p in reversed(range(LINE - 1)):
            store[p] = jnp.broadcast_to(v, (8, ns))
            v = col_mv(v, maps[p]) + buf[p, pl.ds(0, 1), :]
        total = jnp.sum(buf[:, 1:2, :], axis=0)
        return v, total

    run(x_maps[:4])

    def backward(i, v):
        k = top - i
        after[pl.ds(k, 1), :] = v
        return col_mv(v, am[k]) + sources[pl.ds(k, 1), :]

    lax.fori_loop(0, count, backward, jnp.zeros((1, ns), F32))

    arrive(c_line)
    group_costate, totals = line_backward(cz, gz, vloc_z)
    cx[x, pl.ds(0, 1), :] = group_costate
    cx[x, pl.ds(1, 1), :] = totals
    cx[x, pl.ds(2, 6), :] = jnp.zeros((6, ns), F32)
    cx_line = gather_vectors(1, "tm_1", cx)
    run(cx_line)

    def respond(k):
        at = pl.ds(k, 1)
        pull = row_mv(bm[k], after[at, :])
        pulled[at, :] = pull
        step = -row_mv(gm[k], grad_input[at, :] + pull)
        gain[at, :] = step
        pushes[at, :] = col_mv(step, bm[k])

    pl.loop(0, count, unroll=8)(respond)

    def gather_push(k, acc):
        return acc + fold(rst[k] * (pushes[pl.ds(k, 1), :] - defect[pl.ds(k + 1, 1), :]))

    acc = lax.fori_loop(0, top, gather_push, -fold(phi[...] * defect[pl.ds(0, 1), :]), unroll=3)
    f_zero = across(acc) + pushes[pl.ds(top, 1), :]

    relay(x_maps)

    def reach(k):
        w = mm(bm[k], rst[k], 1, 1)
        rows = pl.ds(pl.multiple_of(k * nu, nu), nu)
        wst[rows, :] = w
        gwst[rows, :] = mm(gm[k], w)

    pl.loop(0, top, unroll=5)(reach)
    wst[pl.ds(top * nu, nu), :] = bm[top]
    gwst[pl.ds(top * nu, nu), :] = mm(gm[top], bm[top])

    def gather_reach():
        mmat[...] = mm(wst[...], gwst[...], 0, 0)

    arrive(cx_line)

    arrive(x_maps[2:])
    plane_costate, totals = line_backward(cx, gx, vloc_x)

    down = remote(dy, vy, e_send.at[2], e_recv.at[2], peer("tm_0", LINE - 1))

    @pl.when(y == LINE - 1)
    def _():
        vy[...] = jnp.zeros((8, ns), F32)
        dy[...] = jnp.broadcast_to(plane_costate, (8, ns))
        down.start()

    omega[...] = line_products(gx, sx, px)

    second = [remote(omega.at[r], om1.at[r], y_send.at[n], y_recv.at[n], peer("tm_0", 1)) for n, r in enumerate((high, low))]
    third = [remote(omega.at[r], om2.at[r], y_send.at[2 + n], y_recv.at[2 + n], peer("tm_0", 1)) for n, r in enumerate((high, low))]
    passed = [remote(om1.at[r], om1.at[r], y_send.at[4 + n], y_recv.at[4 + n], peer("tm_0", 1)) for n, r in enumerate((high, low))]

    @pl.when(y == 1)
    def _():
        run(second)

    @pl.when(y == 2)
    def _():
        run(third)

    sy[y] = jnp.broadcast_to(totals, (8, ns))
    s_line = gather_vectors(2, "tm_0", sy)
    run(s_line)
    line_rest(gz, sz, pz)
    line_rest(gx, sx, px)
    tback[...] = mm(sx[x], sz[z])
    t_zero = col_mv(vloc_x[x, pl.ds(0, 1), :], sz[z]) + vloc_z[z, pl.ds(0, 1), :]

    pl.when(y == 0)(gather_reach)

    @pl.when(y < LINE - 1)
    def _():
        down.wait_recv()

    plane_in = vy[pl.ds(0, 1), :]

    @pl.when((y > 0) & (y < LINE - 1))
    def _():
        dy[...] = jnp.broadcast_to(col_mv(plane_in, omega[...]) + plane_costate, (8, ns))
        down.start()

    pl.when(y > 0)(gather_reach)

    v = col_mv(plane_in, tback[...]) + t_zero
    f_own = f_zero - row_mv(mmat[...], v)
    here = x * LINE + z
    plane[here, pl.ds(0, 1), :] = row_mv(tback[...], f_own)
    plane[here, pl.ds(1, 1), :] = row_mv(sz[z], f_own)
    plane[here, pl.ds(2, 1), :] = f_own
    plane[here, pl.ds(3, 1), :] = f_own
    rows = pl.ds(0, 4)
    plane_line = [
        remote(plane.at[here, rows], plane.at[here, rows], p_send.at[n], p_recv.at[n], in_plane(i, j))
        for n, (i, j) in enumerate(offsets)
    ]
    run(plane_line)

    vc = as_column(v)

    def lift(k):
        at = pl.ds(k, 1)
        after[at, :] = after[at, :] + col_apply(vc, rst[k])

    pl.loop(0, top, unroll=5)(lift)
    after[pl.ds(top, 1), :] = v
    before_first = col_apply(vc, phi[...]) + cvec[pl.ds(0, 1), :]

    pl.loop(0, count, unroll=8)(respond)

    arrive(plane_line)
    plane_state = jnp.sum(plane[:, 0:1, :], axis=0)
    fy[y] = jnp.broadcast_to(plane_state, (8, ns))
    ahead = [
        remote(fy.at[y], fy.at[y], f_send.at[by - 1], f_recv.at[by - 1], peer("tm_0", by)) for by in range(1, LINE)
    ]
    for by in range(1, LINE):
        @pl.when(y + by < LINE)
        def _(by=by):
            ahead[by - 1].start()

    @pl.when(y == 2)
    def _():
        for n in range(2):
            second[n].wait_recv()
            passed[n].start()

    def forward(k, carried):
        correction = carried - defect[pl.ds(k, 1), :]
        state_step[pl.ds(k, 1), :] = correction
        return row_mv(am[k], correction) + pushes[pl.ds(k, 1), :]

    lax.fori_loop(0, count, forward, jnp.zeros((1, ns), F32))

    tforw[...] = mm(pz[z], px[x])

    def line_state(vector, maps, at):
        entering = jnp.zeros((1, ns), F32)
        found = entering
        for p in range(LINE - 1):
            entering = row_mv(maps[p], entering) + vector(p) if p else vector(p)
            found = jnp.where(at == p + 1, entering, found)
        return found

    in_line = line_state(lambda p: plane[x * LINE + p, pl.ds(2, 1), :], gz, z)
    groups = [jnp.sum(plane[LINE * p : LINE * p + LINE, 1:2, :], axis=0) for p in range(LINE)]
    in_group = line_state(lambda p: groups[p], gx, x)
    x_zero = row_mv(pz[z], in_group) + in_line

    for by in range(1, LINE):
        @pl.when(y >= by)
        def _(by=by):
            ahead[by - 1].wait_recv()

    @pl.when(y == 0)
    def _():
        dy[...] = jnp.zeros((8, ns), F32)

    def enter(vector):
        dy[...] = jnp.broadcast_to(vector, (8, ns))

    at_plane = lambda p: fy[p, pl.ds(0, 1), :]

    @pl.when(y == 1)
    def _():
        down.wait_send()
        enter(at_plane(0))

    @pl.when(y == 2)
    def _():
        down.wait_send()
        enter(row_mv(om1[...], at_plane(0)) + at_plane(1))

    @pl.when(y == LINE - 1)
    def _():
        down.wait_send()
        arrive(third)
        arrive(passed)
        enter(row_mv(om2[...], row_mv(om1[...], at_plane(0)) + at_plane(1)) + at_plane(2))

    x_in = row_mv(tforw[...], dy[pl.ds(0, 1), :]) + x_zero
    xc = as_column(x_in)
    out_x, out_m = pl.ds(0, count), pl.ds(count, count)
    packed[pl.ds(0, 1), :] = state_step[pl.ds(0, 1), :] + x_in

    def settle(k):
        at = pl.ds(k, 1)
        packed[at, :] = state_step[at, :] + col_apply(xc, qt[k])

    pl.loop(1, count, unroll=5)(settle)

    def close(k):
        at = pl.ds(k, 1)
        now = packed[at, :]
        sources[at, :] = row_mv(vm[k], now - defect[at, :])
        input_linear[at, :] = row_mv(fm[k], now)

    pl.loop(0, count, unroll=8)(close)
    packed[pl.ds(count + 1, top), :] = sources[pl.ds(1, top), :] + after[pl.ds(0, top), :]
    packed[pl.ds(count, 1), :] = sources[pl.ds(0, 1), :] + before_first
    chosen = active[...].astype(F32)
    step = (1.0 - chosen) * (input_linear[...] + gain[...]) + chosen * (upper[...] - inputs[...])
    packed[pl.ds(2 * count, count), pl.ds(0, nu)] = step
    weighted = lax.dot_general(
        step, iw[...], (((1,), (1,)), ((), ())), precision=PRECISE, preferred_element_type=F32
    )
    packed[pl.ds(2 * count, count), pl.ds(HALF, nu)] = chosen * (grad_input[...] + weighted + pulled[...])

    arrive(s_line)
    totals = jnp.sum(sy[:, 0:1, :], axis=0)
    horizon = count * LINE**3
    pick = lambda n: jnp.sum(jnp.where(lane == n, totals, 0.0), axis=1, keepdims=True)
    primal = pick(0) / (pick(3) + floor_share * horizon * ns)
    dual = pick(1) / (pick(4) + floor_share * horizon * (ns + nu))
    complement = pick(2) / (pick(5) + floor_share * horizon * nu)
    lanes = lax.broadcasted_iota(jnp.int32, (8, ns), 1)
    values = jnp.where(lanes == 0, primal, jnp.where(lanes == 1, dual, complement))
    packed[pl.ds(3 * count, 8), :] = jnp.sqrt(values)

    for copy in [to_prev, to_next] + z_maps + x_maps + c_line + cx_line + plane_line + s_line:
        copy.wait_send()

    for by in range(1, LINE):
        @pl.when(y + by < LINE)
        def _(by=by):
            ahead[by - 1].wait_send()

    @pl.when(y == 1)
    def _():
        for copy in second:
            copy.wait_send()

    @pl.when(y == 2)
    def _():
        for copy in third + passed:
            copy.wait_send()


def unpack(packed, state_step, input_step, multiplier_step, bound_step, norms):
    count, nu = input_step.shape
    state_step[...] = packed[pl.ds(0, count), :]
    multiplier_step[...] = packed[pl.ds(count, count), :]
    input_step[...] = packed[pl.ds(2 * count, count), pl.ds(0, nu)]
    bound_step[...] = packed[pl.ds(2 * count, count), pl.ds(HALF, nu)]
    norms[...] = packed[pl.ds(3 * count, 1), pl.ds(0, HALF)][0, :3]


def local(*args):
    states, inputs = args[12], args[13]
    count, ns = states.shape
    nu = inputs.shape[1]
    v = lambda *shape: pltpu.VMEM(shape, F32)
    dma = lambda *shape: pltpu.SemaphoreType.DMA(shape)
    square = v(ns, ns)
    line = v(LINE, ns, ns)
    rows = v(LINE, 8, ns)
    row = v(8, ns)
    wide, narrow = v(count, ns), v(count, nu)
    scratch = [
        v(count, ns, ns), v(count, nu, ns), v(count, ns, ns), v(count, nu, ns), v(count, ns, ns),
        v(count, nu, nu), v(nu, nu), wide, wide, narrow, wide, narrow,
        wide, narrow, wide, narrow, pltpu.VMEM((count, nu), jnp.int32),
        v(count, ns, ns), v(count, ns, ns), v(count // 2, ns, ns), square, square, v(count * nu, ns), v(count * nu, ns),
        line, line, line, line, line, line, square, square, square, square, square,
        wide, wide, wide, wide, narrow, wide, wide, narrow, narrow, wide, wide,
        row, row, row, rows, rows, v(LINE * LINE, 8, ns), rows, row, row, rows,
        rows, rows, row,
        dma(18), dma(count), dma(2, 6), dma(2, 6), dma(3, LINE - 1), dma(3, LINE - 1), dma(3), dma(3),
        dma(LINE * LINE - 1), dma(LINE * LINE - 1), dma(6), dma(6), dma(LINE - 1), dma(LINE - 1),
    ]
    vmem = pl.BlockSpec(memory_space=pltpu.VMEM)
    packed = pl.pallas_call(
        kernel,
        out_shape=pltpu.VMEM((3 * count + 8, ns), F32),
        in_specs=[pl.BlockSpec(memory_space=pl.ANY)] * len(args),
        out_specs=vmem,
        scratch_shapes=scratch,
        compiler_params=pltpu.CompilerParams(
            collective_id=0, has_side_effects=True, vmem_limit_bytes=56 * 1024 * 1024
        ),
        name="riccati",
    )(*args)
    return pl.pallas_call(
        unpack,
        out_shape=[
            jax.ShapeDtypeStruct((count, ns), F32),
            jax.ShapeDtypeStruct((count, nu), F32),
            jax.ShapeDtypeStruct((count, ns), F32),
            jax.ShapeDtypeStruct((count, nu), F32),
            jax.ShapeDtypeStruct((3,), F32),
        ],
        in_specs=[vmem],
        out_specs=[vmem] * 5,
        name="unpack",
    )(pltpu.with_memory_space_constraint(packed, pltpu.VMEM))


def solution(mesh):
    lines = Mesh(
        mesh.devices.reshape(LINE, LINE, LINE, mesh.shape["batch"]), ("tm_0", "tm_1", "tm_2", "batch")
    )
    cube, flat = P(BATCH_TM, None, None), P(BATCH_TM, None)
    return jax.shard_map(
        local,
        mesh=lines,
        in_specs=(cube,) * 6 + (P("batch", None),) + (flat,) * 10,
        out_specs=(flat, flat, flat, flat, P("batch")),
        check_vma=False,
    )
```

time: 87.3 us -> 52.1 us (0.60)
  Pallas kernels: 79.7 us -> 51.1 us
  local copies, waits for them, and re-layouts: 6.43 us -> 0 us
    pallas_call x1 -> x2, Pallas kernels: 79.7 us -> 51.1 us  [the longest x1 50.5 us: local(): pl.pallas_call(kernel, out_shape=pltpu.VMEM((3 * count + 8, ns), F32), in...]
    unnamed x4 -> x0, local copies, waits for them, and re-layouts: 5.23 us -> none
    squeeze x1 -> x0, local copies, waits for them, and re-layouts: 1.19 us -> none  [local(): return (*out[:4], out[4][0, :3])]
where the time goes in v2:
time: 52.1 us; the launch traced here: 51.7 us
  Pallas kernels  51.1 us (98%)
  between operations  0.65 us (1%)
    pallas_call x1, Pallas kernels, local(): pl.pallas_call(kernel, out_shape=pltpu.VMEM((3 * count + 8, ns), F32), in...  50.5 us

profile of v2, /device:TPU:24, one launch (start us, length us, event | category | flops | bytes accessed | tf_op | source)
XLA Modules:
  0.0 51.7 jit_solution(438782245762775000)
XLA Ops:
  0.6 50.5 %riccati.1.packed = f32[56,256]{1,0:T(8,128)S(1)} custom-call(f32[16,256,256]{2,1,0:T(8,128)} %state_map_h.1, f32[16,64,256]{2,1,0:T(8,128)} %input_map_h.1, f32[16,256,256]{2,1,0:T(8,128)} %closed_loop_h.1, f32[16,64,256]{2,1,0:T(8,128)} %feedback_h.1, f32[16,256,256]{2,1,0:T(8,128)} %value_h.1, f32[16,64,64]{2,1,0:T(8,128)} %gain_h.1, f32[64,64]{1,0:T(8,128)} %weight_h.1, ...), custom_call_target="tpu_custom_call" | custom-call | tf_op jit(solution)/shard_map/riccati/pallas_call | solution.py:593
  51.1 0.6 %unpack.1 = (f32[16,256]{1,0:T(8,128)}, f32[16,64]{1,0:T(8,128)}, f32[16,256]{1,0:T(8,128)}, f32[16,64]{1,0:T(8,128)}, f32[3]{0:T(128)}) custom-call(f32[56,256]{1,0:T(8,128)S(1)} %riccati.1.packed), custom_call_target="tpu_custom_call" | custom-call | tf_op jit(solution)/shard_map/unpack/pallas_call | solution.py:604

commit v3 on v2

--- a/solution.py
+++ b/solution.py
@@ -91,16 +91,17 @@
     packed,
     sm, bm, am, fm, vm, gm, iw, state_weight, state_linear, input_linear, offset, upper,
     states, inputs, mult, bound, active,
-    rst, qt, tree, phi, mmat, wst, gwst,
+    rst, qt, tree, phi, weighted_map, mmat, wst, gwst,
     gz, gx, sz, pz, sx, px, omega, om1, om2, tback, tforw,
     predicted, following, defect, grad_state, grad_input, sources, after, pulled, gain, pushes, state_step,
-    edge, from_next, from_prev, cz, cx, plane, fy, vy, dy, sy,
+    edge, from_next, from_prev, cz, cx, plane_sum, plane_own, fy, vy, dy, entry, fvec, avec, answer, sy,
     vloc_z, vloc_x, cvec,
     in_sem, a_sem, m_send, m_recv, v_send, v_recv, e_send, e_recv, p_send, p_recv, y_send, y_recv, f_send, f_recv,
 ):
     count, ns = states.shape
     nu = inputs.shape[1]
     y, x, z = (lax.axis_index(a) for a in TM)
+    core = lax.axis_index("batch")
     place = (y * LINE + x) * LINE + z
     last = LINE**3 - 1
     top = count - 1
@@ -124,15 +125,23 @@
     def in_plane(i, j):
         return {"tm_1": lax.rem(x + i, LINE), "tm_2": lax.rem(z + j, LINE)}
 
-    a_copies = [pltpu.make_async_copy(closed_loop_h.at[k], am.at[k], a_sem.at[k]) for k in range(count)]
+    first_half, last_half = pl.ds(0, count // 2), pl.ds(count // 2, count // 2)
+    a_copies = [
+        pltpu.make_async_copy(closed_loop_h.at[k], am.at[k], a_sem.at[k // (count // 2)]) for k in range(count)
+    ]
+    a_halves = [
+        pltpu.make_async_copy(closed_loop_h.at[part], am.at[part], a_sem.at[n])
+        for n, part in enumerate((first_half, last_half))
+    ]
     pairs = [
         (states_h, states), (inputs_h, inputs), (input_map_h.at[top], bm.at[top]), (state_map_h.at[top], sm.at[top]),
         (multipliers_h, mult), (input_map_h.at[pl.ds(0, top)], bm.at[pl.ds(0, top)]),
-        (state_map_h.at[pl.ds(0, top)], sm.at[pl.ds(0, top)]), (state_weight_h, state_weight),
+        (state_map_h.at[pl.ds(0, 8)], sm.at[pl.ds(0, 8)]),
+        (state_map_h.at[pl.ds(8, top - 8)], sm.at[pl.ds(8, top - 8)]), (state_weight_h, state_weight),
         (state_linear_h, state_linear), (input_linear_h, input_linear), (offset_h, offset), (upper_h, upper),
         (bound_h, bound), (active_h, active), (weight_h, iw), (value_h, vm), (feedback_h, fm), (gain_h, gm),
     ]
-    in_copies = [pltpu.make_async_copy(s, d, in_sem.at[n]) for n, (s, d) in enumerate(pairs)]
+    in_copies = [pltpu.make_async_copy(s, d, in_sem.at[n if n < 14 else n - 14]) for n, (s, d) in enumerate(pairs)]
     for copy in in_copies[:5]:
         copy.start()
     for copy in a_copies:
@@ -150,11 +159,10 @@
         at = pl.ds(k, 1)
         predicted[at, :] = row_mv(sm[k], states[at, :]) + col_mv(inputs[at, :], bm[k])
 
-    for copy in a_copies[: count // 2]:
-        copy.wait()
+    a_halves[0].wait()
     for i in range(count // 4):
         tree[i] = mm(am[2 * i + 1], am[2 * i])
-    for copy in a_copies[count // 2 :] + in_copies[:5]:
+    for copy in a_halves[1:] + in_copies[:5]:
         copy.wait()
     predict(top)
     edge[...] = jnp.broadcast_to(predicted[pl.ds(top, 1), :], (8, ns))
@@ -175,71 +183,79 @@
             src_ref=src, dst_ref=dst, send_sem=send, recv_sem=recv, device_id=device, device_id_type=MESH
         )
 
-    high, low = pl.ds(0, ns // 2), pl.ds(ns // 2, ns // 2)
+    part = ns // 4
+    high, low = pl.ds(0, 2 * part), pl.ds(2 * part, 2 * part)
+    quarters = [pl.ds(n * part, part) for n in range(4)]
 
     def gather_maps(stage, axis, maps):
         at = spot[axis]
         right, left = peer(axis, 1), peer(axis, LINE - 1)
         before, behind = lax.rem(at + LINE - 1, LINE), lax.rem(at + 1, LINE)
         plan = [
-            (at, high, right), (at, low, left), (at, low, right), (at, high, left),
-            (before, high, right), (behind, low, left),
+            (at, quarters[0], right), (at, quarters[3], left), (at, quarters[1], right), (at, quarters[2], left),
+            (at, low, right), (at, high, left),
+            (before, quarters[0], right), (behind, quarters[3], left),
+            (before, quarters[1], right), (behind, quarters[2], left),
         ]
-        return [
-            remote(maps.at[s, rows], maps.at[s, rows], m_send.at[stage, n], m_recv.at[stage, n], dev)
-            for n, (s, rows, dev) in enumerate(plan)
+        sems = (0, 0, 1, 1, 2, 2, 2, 2, 2, 2)
+        copies = [
+            remote(maps.at[s, rows], maps.at[s, rows], m_send.at[stage], m_recv.at[stage, n], dev)
+            for n, (s, rows, dev) in zip(sems, plan)
         ]
-
-    def relay(copies):
-        copies[0].wait_recv()
-        copies[4].start()
-        copies[1].wait_recv()
-        copies[5].start()
+        whole = remote(maps.at[pl.ds(0, 3)], maps.at[pl.ds(0, 2)], m_send.at[stage], m_recv.at[stage, 2], right)
+        return copies, whole
+
+    def relay(copies, maps, stage, turn):
+        remote(maps.at[0, high], maps.at[0, high], m_send.at[stage], m_recv.at[stage, turn], peer("tm_0", 1)).wait_recv()
+        run(copies[2 * turn + 6 : 2 * turn + 8])
 
     def gather_vectors(stage, axis, buf):
         at = spot[axis]
-        return [
-            remote(buf.at[at], buf.at[at], v_send.at[stage, by - 1], v_recv.at[stage, by - 1], peer(axis, by))
-            for by in range(1, LINE)
+        copies = [
+            remote(buf.at[at], buf.at[at], v_send.at[stage], v_recv.at[stage], peer(axis, by)) for by in range(1, LINE)
         ]
+        three = buf.at[pl.ds(0, LINE - 1)]
+        return copies, remote(three, three, v_send.at[stage], v_recv.at[stage], peer(axis, 1))
 
     def run(copies):
         for copy in copies:
             copy.start()
 
-    def arrive(copies):
-        for copy in copies:
-            copy.wait_recv()
-
     to_prev = remote(mult.at[pl.ds(0, 8)], from_next, e_send.at[0], e_recv.at[0], prev_device)
     to_next = remote(edge, from_prev, e_send.at[1], e_recv.at[1], next_device)
-    z_maps = gather_maps(0, "tm_2", gz)
-    run([to_prev, to_next] + z_maps[:4])
-
+    z_maps, z_all = gather_maps(0, "tm_2", gz)
+    run([to_prev, to_next])
     half = count // 2
-    rst[top - 1] = am[top]
-    rst[top - 2] = tree[half - 1]
+
+    @pl.when(core == 0)
+    def _():
+        run(z_maps[:6])
+
     qt[1] = jnp.transpose(am[0])
     qt[2] = jnp.transpose(tree[0])
 
-    def chain_step(i):
-        j = half - 1 - i
-        suffix, prefix = rst[2 * j + 1], qt[2 * i]
-        rst[2 * j] = mm(suffix, am[2 * j + 1])
-        rst[2 * j - 1] = mm(suffix, tree[j])
+    def prefix_step(i):
+        prefix = qt[2 * i]
         qt[2 * i + 1] = mm(prefix, am[2 * i], 1, 1)
         qt[2 * i + 2] = mm(prefix, tree[i], 1, 1)
 
-    pl.loop(1, half - 1)(chain_step)
-    rst[0] = mm(rst[1], am[1])
+    pl.loop(1, half - 1)(prefix_step)
     qt[top] = mm(qt[top - 1], am[top - 1], 1, 1)
 
-    for copy in in_copies[5:]:
+    @pl.when(core == 0)
+    def _():
+        relay(z_maps, gz, 0, 0)
+
+    for copy in in_copies[5:8]:
         copy.wait()
     pl.loop(0, top, unroll=5)(predict)
 
-    relay(z_maps)
-
+    @pl.when(core == 0)
+    def _():
+        relay(z_maps, gz, 0, 1)
+
+    for copy in in_copies[8:16]:
+        copy.wait()
     to_prev.wait_recv()
     following[pl.ds(0, top), :] = mult[pl.ds(1, top), :]
     following[pl.ds(top, 1), :] = jnp.where(place == last, 0.0, from_next[pl.ds(0, 1), :])
@@ -257,6 +273,12 @@
     )
     grad_input[...] = weighted + input_linear[...] - grad_input[...] + bound[...]
 
+    @pl.when(core == 1)
+    def _():
+        run(z_maps[:6])
+
+    for copy in in_copies[16:]:
+        copy.wait()
     to_next.wait_recv()
     defect[pl.ds(1, top), :] = states[pl.ds(1, top), :] - predicted[pl.ds(0, top), :] - offset[pl.ds(1, top), :]
     entered = jnp.where(place == 0, 0.0, from_prev[pl.ds(0, 1), :])
@@ -265,8 +287,15 @@
     def source(k):
         at = pl.ds(k, 1)
         sources[at, :] = row_mv(vm[k], defect[at, :]) + grad_state[at, :] + col_mv(grad_input[at, :], fm[k])
+        weighted_map[k] = mm(gm[k], bm[k])
 
     pl.loop(0, count, unroll=4)(source)
+
+    @pl.when(core == 1)
+    def _():
+        relay(z_maps, gz, 0, 0)
+        relay(z_maps, gz, 0, 1)
+
 
     def gather_source(k, acc):
         return acc + fold(qt[k] * sources[pl.ds(k, 1), :])
@@ -289,12 +318,12 @@
     cz[z, pl.ds(0, 1), :] = local_costate
     cz[z, pl.ds(1, 1), :] = stats
     cz[z, pl.ds(2, 6), :] = jnp.zeros((6, ns), F32)
-    c_line = gather_vectors(0, "tm_2", cz)
+    c_line, c_all = gather_vectors(0, "tm_2", cz)
     run(c_line)
 
-    arrive(z_maps[2:])
+    z_all.wait_recv()
     gx[x] = line_products(gz, sz, pz)
-    x_maps = gather_maps(1, "tm_1", gx)
+    x_maps, x_all = gather_maps(1, "tm_1", gx)
 
     def line_backward(buf, maps, store):
         v = buf[LINE - 1, pl.ds(0, 1), :]
@@ -305,22 +334,38 @@
         total = jnp.sum(buf[:, 1:2, :], axis=0)
         return v, total
 
-    run(x_maps[:4])
+    run(x_maps[:6])
+
+    rst[top - 1] = am[top]
+    rst[top - 2] = tree[half - 1]
+
+    def suffix_step(i):
+        j = half - 1 - i
+        suffix = rst[2 * j + 1]
+        rst[2 * j] = mm(suffix, am[2 * j + 1])
+        rst[2 * j - 1] = mm(suffix, tree[j])
+
+    pl.loop(1, half - 1)(suffix_step)
+    rst[0] = mm(rst[1], am[1])
+
+    c_all.wait_recv()
+    group_costate, totals = line_backward(cz, gz, vloc_z)
+    cx[x, pl.ds(0, 1), :] = group_costate
+    cx[x, pl.ds(1, 1), :] = totals
+    cx[x, pl.ds(2, 6), :] = jnp.zeros((6, ns), F32)
+    cx_line, cx_all = gather_vectors(1, "tm_1", cx)
+    run(cx_line)
+
+    relay(x_maps, gx, 1, 0)
 
     def backward(i, v):
         k = top - i
         after[pl.ds(k, 1), :] = v
         return col_mv(v, am[k]) + sources[pl.ds(k, 1), :]
 
-    lax.fori_loop(0, count, backward, jnp.zeros((1, ns), F32))
-
-    arrive(c_line)
-    group_costate, totals = line_backward(cz, gz, vloc_z)
-    cx[x, pl.ds(0, 1), :] = group_costate
-    cx[x, pl.ds(1, 1), :] = totals
-    cx[x, pl.ds(2, 6), :] = jnp.zeros((6, ns), F32)
-    cx_line = gather_vectors(1, "tm_1", cx)
-    run(cx_line)
+    v = lax.fori_loop(0, half, backward, jnp.zeros((1, ns), F32))
+    relay(x_maps, gx, 1, 1)
+    lax.fori_loop(half, count, backward, v)
 
     def respond(k):
         at = pl.ds(k, 1)
@@ -330,47 +375,51 @@
         gain[at, :] = step
         pushes[at, :] = col_mv(step, bm[k])
 
-    pl.loop(0, count, unroll=8)(respond)
-
     def gather_push(k, acc):
         return acc + fold(rst[k] * (pushes[pl.ds(k, 1), :] - defect[pl.ds(k + 1, 1), :]))
 
-    acc = lax.fori_loop(0, top, gather_push, -fold(phi[...] * defect[pl.ds(0, 1), :]), unroll=3)
-    f_zero = across(acc) + pushes[pl.ds(top, 1), :]
-
-    relay(x_maps)
+    def local_state():
+        pl.loop(0, count, unroll=8)(respond)
+        acc = lax.fori_loop(0, top, gather_push, -fold(phi[...] * defect[pl.ds(0, 1), :]), unroll=3)
+        fvec[...] = jnp.broadcast_to(across(acc) + pushes[pl.ds(top, 1), :], (8, ns))
+
+    local_state()
 
     def reach(k):
-        w = mm(bm[k], rst[k], 1, 1)
+        both = jnp.concatenate([bm[k], weighted_map[k]], axis=0)
+        w = mm(both, rst[k], 1, 1)
         rows = pl.ds(pl.multiple_of(k * nu, nu), nu)
-        wst[rows, :] = w
-        gwst[rows, :] = mm(gm[k], w)
-
-    pl.loop(0, top, unroll=5)(reach)
-    wst[pl.ds(top * nu, nu), :] = bm[top]
-    gwst[pl.ds(top * nu, nu), :] = mm(gm[top], bm[top])
+        wst[rows, :] = w[:nu]
+        gwst[rows, :] = w[nu:]
 
     def gather_reach():
+        pl.loop(0, top, unroll=5)(reach)
+        wst[pl.ds(top * nu, nu), :] = bm[top]
+        gwst[pl.ds(top * nu, nu), :] = weighted_map[top]
         mmat[...] = mm(wst[...], gwst[...], 0, 0)
 
-    arrive(cx_line)
-
-    arrive(x_maps[2:])
+    cx_all.wait_recv()
+
+    x_all.wait_recv()
     plane_costate, totals = line_backward(cx, gx, vloc_x)
 
     down = remote(dy, vy, e_send.at[2], e_recv.at[2], peer("tm_0", LINE - 1))
 
     @pl.when(y == LINE - 1)
     def _():
-        vy[...] = jnp.zeros((8, ns), F32)
         dy[...] = jnp.broadcast_to(plane_costate, (8, ns))
         down.start()
 
     omega[...] = line_products(gx, sx, px)
 
-    second = [remote(omega.at[r], om1.at[r], y_send.at[n], y_recv.at[n], peer("tm_0", 1)) for n, r in enumerate((high, low))]
-    third = [remote(omega.at[r], om2.at[r], y_send.at[2 + n], y_recv.at[2 + n], peer("tm_0", 1)) for n, r in enumerate((high, low))]
-    passed = [remote(om1.at[r], om1.at[r], y_send.at[4 + n], y_recv.at[4 + n], peer("tm_0", 1)) for n, r in enumerate((high, low))]
+    halves = (high, low)
+    second = [remote(omega.at[r], om1.at[r], y_send.at[0], y_recv.at[n], peer("tm_0", 1)) for n, r in enumerate(halves)]
+    third = remote(omega, om2, y_send.at[0], y_recv.at[2], peer("tm_0", 1))
+    passed = [remote(om1.at[r], om1.at[r], y_send.at[1], y_recv.at[n], peer("tm_0", 1)) for n, r in enumerate(halves)]
+
+    def pass_on(n):
+        second[n].wait_recv()
+        passed[n].start()
 
     @pl.when(y == 1)
     def _():
@@ -378,17 +427,32 @@
 
     @pl.when(y == 2)
     def _():
-        run(third)
+        third.start()
 
     sy[y] = jnp.broadcast_to(totals, (8, ns))
-    s_line = gather_vectors(2, "tm_0", sy)
+    s_line, s_all = gather_vectors(2, "tm_0", sy)
     run(s_line)
     line_rest(gz, sz, pz)
     line_rest(gx, sx, px)
     tback[...] = mm(sx[x], sz[z])
     t_zero = col_mv(vloc_x[x, pl.ds(0, 1), :], sz[z]) + vloc_z[z, pl.ds(0, 1), :]
 
-    pl.when(y == 0)(gather_reach)
+    def combine():
+        inward = mm(tback[...], mmat[...])
+        answer[...] = mm(inward, tback[...], 1, 1)
+        constant = row_mv(tback[...], fvec[pl.ds(0, 1), :]) - row_mv(inward, t_zero)
+        avec[...] = jnp.broadcast_to(constant, (8, ns))
+
+    @pl.when(y == 0)
+    def _():
+        gather_reach()
+        combine()
+
+    pl.when(y == 1)(gather_reach)
+
+    @pl.when(y == LINE - 1)
+    def _():
+        vy[...] = jnp.zeros((8, ns), F32)
 
     @pl.when(y < LINE - 1)
     def _():
@@ -396,26 +460,37 @@
 
     plane_in = vy[pl.ds(0, 1), :]
 
-    @pl.when((y > 0) & (y < LINE - 1))
+    @pl.when((y == 1) | (y == 2))
     def _():
         dy[...] = jnp.broadcast_to(col_mv(plane_in, omega[...]) + plane_costate, (8, ns))
         down.start()
 
-    pl.when(y > 0)(gather_reach)
-
+    @pl.when(y > 1)
+    def _():
+        gather_reach()
+
+    pl.when(y > 0)(combine)
+
+    here = x * LINE + z
+    plane_sum[here, pl.ds(0, 1), :] = avec[pl.ds(0, 1), :] - row_mv(answer[...], plane_in)
+
+    def to_plane(buf, rows, n):
+        return [
+            remote(buf.at[here, rows], buf.at[here, rows], p_send.at[n], p_recv.at[n], in_plane(i, j)) for i, j in offsets
+        ]
+
+    sum_rows, own_rows = pl.ds(0, 1), pl.ds(0, 2)
+    run(to_plane(plane_sum, sum_rows, 0))
     v = col_mv(plane_in, tback[...]) + t_zero
-    f_own = f_zero - row_mv(mmat[...], v)
-    here = x * LINE + z
-    plane[here, pl.ds(0, 1), :] = row_mv(tback[...], f_own)
-    plane[here, pl.ds(1, 1), :] = row_mv(sz[z], f_own)
-    plane[here, pl.ds(2, 1), :] = f_own
-    plane[here, pl.ds(3, 1), :] = f_own
-    rows = pl.ds(0, 4)
-    plane_line = [
-        remote(plane.at[here, rows], plane.at[here, rows], p_send.at[n], p_recv.at[n], in_plane(i, j))
-        for n, (i, j) in enumerate(offsets)
-    ]
-    run(plane_line)
+    f_own = fvec[pl.ds(0, 1), :] - row_mv(mmat[...], v)
+    plane_own[here, pl.ds(0, 1), :] = row_mv(sz[z], f_own)
+    plane_own[here, pl.ds(1, 1), :] = f_own
+    run(to_plane(plane_own, own_rows, 1))
+    others = pl.ds(0, LINE * LINE - 1)
+    sum_line = remote(plane_sum.at[others, sum_rows], plane_sum.at[others, sum_rows], p_send.at[0], p_recv.at[0], peer("tm_1", 1))
+    own_line = remote(plane_own.at[others, own_rows], plane_own.at[others, own_rows], p_send.at[1], p_recv.at[1], peer("tm_1", 1))
+
+    pl.when(y == 2)(lambda: pass_on(0))
 
     vc = as_column(v)
 
@@ -429,8 +504,17 @@
 
     pl.loop(0, count, unroll=8)(respond)
 
-    arrive(plane_line)
-    plane_state = jnp.sum(plane[:, 0:1, :], axis=0)
+    pl.when(y == 2)(lambda: pass_on(1))
+
+    def forward(k, carried):
+        correction = carried - defect[pl.ds(k, 1), :]
+        state_step[pl.ds(k, 1), :] = correction
+        return row_mv(am[k], correction) + pushes[pl.ds(k, 1), :]
+
+    lax.fori_loop(0, count, forward, jnp.zeros((1, ns), F32))
+
+    sum_line.wait_recv()
+    plane_state = jnp.sum(plane_sum[:, 0:1, :], axis=0)
     fy[y] = jnp.broadcast_to(plane_state, (8, ns))
     ahead = [
         remote(fy.at[y], fy.at[y], f_send.at[by - 1], f_recv.at[by - 1], peer("tm_0", by)) for by in range(1, LINE)
@@ -440,19 +524,7 @@
         def _(by=by):
             ahead[by - 1].start()
 
-    @pl.when(y == 2)
-    def _():
-        for n in range(2):
-            second[n].wait_recv()
-            passed[n].start()
-
-    def forward(k, carried):
-        correction = carried - defect[pl.ds(k, 1), :]
-        state_step[pl.ds(k, 1), :] = correction
-        return row_mv(am[k], correction) + pushes[pl.ds(k, 1), :]
-
-    lax.fori_loop(0, count, forward, jnp.zeros((1, ns), F32))
-
+    own_line.wait_recv()
     tforw[...] = mm(pz[z], px[x])
 
     def line_state(vector, maps, at):
@@ -463,8 +535,8 @@
             found = jnp.where(at == p + 1, entering, found)
         return found
 
-    in_line = line_state(lambda p: plane[x * LINE + p, pl.ds(2, 1), :], gz, z)
-    groups = [jnp.sum(plane[LINE * p : LINE * p + LINE, 1:2, :], axis=0) for p in range(LINE)]
+    in_line = line_state(lambda p: plane_own[x * LINE + p, pl.ds(1, 1), :], gz, z)
+    groups = [jnp.sum(plane_own[LINE * p : LINE * p + LINE, 0:1, :], axis=0) for p in range(LINE)]
     in_group = line_state(lambda p: groups[p], gx, x)
     x_zero = row_mv(pz[z], in_group) + in_line
 
@@ -475,31 +547,29 @@
 
     @pl.when(y == 0)
     def _():
-        dy[...] = jnp.zeros((8, ns), F32)
+        entry[...] = jnp.zeros((8, ns), F32)
 
     def enter(vector):
-        dy[...] = jnp.broadcast_to(vector, (8, ns))
+        entry[...] = jnp.broadcast_to(vector, (8, ns))
 
     at_plane = lambda p: fy[p, pl.ds(0, 1), :]
 
     @pl.when(y == 1)
     def _():
-        down.wait_send()
         enter(at_plane(0))
 
     @pl.when(y == 2)
     def _():
-        down.wait_send()
         enter(row_mv(om1[...], at_plane(0)) + at_plane(1))
 
     @pl.when(y == LINE - 1)
     def _():
-        down.wait_send()
-        arrive(third)
-        arrive(passed)
+        third.wait_recv()
+        for copy in passed:
+            copy.wait_recv()
         enter(row_mv(om2[...], row_mv(om1[...], at_plane(0)) + at_plane(1)) + at_plane(2))
 
-    x_in = row_mv(tforw[...], dy[pl.ds(0, 1), :]) + x_zero
+    x_in = row_mv(tforw[...], entry[pl.ds(0, 1), :]) + x_zero
     xc = as_column(x_in)
     out_x, out_m = pl.ds(0, count), pl.ds(count, count)
     packed[pl.ds(0, 1), :] = state_step[pl.ds(0, 1), :] + x_in
@@ -527,7 +597,7 @@
     )
     packed[pl.ds(2 * count, count), pl.ds(HALF, nu)] = chosen * (grad_input[...] + weighted + pulled[...])
 
-    arrive(s_line)
+    s_all.wait_recv()
     totals = jnp.sum(sy[:, 0:1, :], axis=0)
     horizon = count * LINE**3
     pick = lambda n: jnp.sum(jnp.where(lane == n, totals, 0.0), axis=1, keepdims=True)
@@ -538,7 +608,7 @@
     values = jnp.where(lanes == 0, primal, jnp.where(lanes == 1, dual, complement))
     packed[pl.ds(3 * count, 8), :] = jnp.sqrt(values)
 
-    for copy in [to_prev, to_next] + z_maps + x_maps + c_line + cx_line + plane_line + s_line:
+    for copy in [to_prev, to_next, z_all, x_all, c_all, cx_all, s_all, sum_line, own_line]:
         copy.wait_send()
 
     for by in range(1, LINE):
@@ -546,15 +616,17 @@
         def _(by=by):
             ahead[by - 1].wait_send()
 
-    @pl.when(y == 1)
-    def _():
-        for copy in second:
-            copy.wait_send()
+    @pl.when((y == 1) | (y == 2))
+    def _():
+        third.wait_send()
 
     @pl.when(y == 2)
     def _():
-        for copy in third + passed:
-            copy.wait_send()
+        remote(om1, om1, y_send.at[1], y_recv.at[0], peer("tm_0", 1)).wait_send()
+
+    @pl.when(y > 0)
+    def _():
+        down.wait_send()
 
 
 def unpack(packed, state_step, input_step, multiplier_step, bound_step, norms):
@@ -581,13 +653,13 @@
         v(count, ns, ns), v(count, nu, ns), v(count, ns, ns), v(count, nu, ns), v(count, ns, ns),
         v(count, nu, nu), v(nu, nu), wide, wide, narrow, wide, narrow,
         wide, narrow, wide, narrow, pltpu.VMEM((count, nu), jnp.int32),
-        v(count, ns, ns), v(count, ns, ns), v(count // 2, ns, ns), square, square, v(count * nu, ns), v(count * nu, ns),
+        v(count, ns, ns), v(count, ns, ns), v(count // 2, ns, ns), square, v(count, nu, ns), square, v(count * nu, ns), v(count * nu, ns),
         line, line, line, line, line, line, square, square, square, square, square,
         wide, wide, wide, wide, narrow, wide, wide, narrow, narrow, wide, wide,
-        row, row, row, rows, rows, v(LINE * LINE, 8, ns), rows, row, row, rows,
+        row, row, row, rows, rows, v(LINE * LINE, 8, ns), v(LINE * LINE, 8, ns), rows, row, row, row, row, row, square, rows,
         rows, rows, row,
-        dma(18), dma(count), dma(2, 6), dma(2, 6), dma(3, LINE - 1), dma(3, LINE - 1), dma(3), dma(3),
-        dma(LINE * LINE - 1), dma(LINE * LINE - 1), dma(6), dma(6), dma(LINE - 1), dma(LINE - 1),
+        dma(14), dma(2), dma(2), dma(2, 3), dma(3), dma(3), dma(3), dma(3),
+        dma(2), dma(2), dma(2), dma(3), dma(LINE - 1), dma(LINE - 1),
     ]
     vmem = pl.BlockSpec(memory_space=pltpu.VMEM)
     packed = pl.pallas_call(

time: 52.1 us -> 48.4 us (0.929)
  Pallas kernels: 51.1 us -> 47.5 us
    pallas_call x1, Pallas kernels: 50.5 us -> 46.9 us  [local(): pl.pallas_call(kernel, out_shape=pltpu.VMEM((3 * count + 8, ns), F32), in...]
where the time goes in v3:
time: 48.4 us; the launch traced here: 48.2 us
  Pallas kernels  47.5 us (98%)
  between operations  0.65 us (1%)
    pallas_call x1, Pallas kernels, local(): pl.pallas_call(kernel, out_shape=pltpu.VMEM((3 * count + 8, ns), F32), in...  46.9 us

profile of v3, /device:TPU:24, one launch (start us, length us, event | category | flops | bytes accessed | tf_op | source)
XLA Modules:
  0.0 48.2 jit_solution(17000181107239855283)
XLA Ops:
  0.6 46.9 %riccati.1.packed = f32[56,256]{1,0:T(8,128)S(1)} custom-call(f32[16,256,256]{2,1,0:T(8,128)} %state_map_h.1, f32[16,64,256]{2,1,0:T(8,128)} %input_map_h.1, f32[16,256,256]{2,1,0:T(8,128)} %closed_loop_h.1, f32[16,64,256]{2,1,0:T(8,128)} %feedback_h.1, f32[16,256,256]{2,1,0:T(8,128)} %value_h.1, f32[16,64,64]{2,1,0:T(8,128)} %gain_h.1, f32[64,64]{1,0:T(8,128)} %weight_h.1, ...), custom_call_target="tpu_custom_call" | custom-call | tf_op jit(solution)/shard_map/riccati/pallas_call | solution.py:665
  47.5 0.6 %unpack.1 = (f32[16,256]{1,0:T(8,128)}, f32[16,64]{1,0:T(8,128)}, f32[16,256]{1,0:T(8,128)}, f32[16,64]{1,0:T(8,128)}, f32[3]{0:T(128)}) custom-call(f32[56,256]{1,0:T(8,128)S(1)} %riccati.1.packed), custom_call_target="tpu_custom_call" | custom-call | tf_op jit(solution)/shard_map/unpack/pallas_call | solution.py:676

commit v4 on v3

--- a/solution.py
+++ b/solution.py
@@ -115,6 +115,7 @@
 
     next_device = device_at(lax.rem(place + 1, last + 1))
     prev_device = device_at(lax.rem(place + last, last + 1))
+    has_next, has_prev = pl.when(place < last), pl.when(place > 0)
     spot = {"tm_0": y, "tm_1": x, "tm_2": z}
 
     def peer(axis, by):
@@ -152,8 +153,8 @@
         pl.semaphore_signal(barrier, inc=1, device_id=peer("tm_0", by), device_id_type=MESH)
     for i, j in offsets:
         pl.semaphore_signal(barrier, inc=1, device_id=in_plane(i, j), device_id_type=MESH)
-    for device in (next_device, prev_device):
-        pl.semaphore_signal(barrier, inc=1, device_id=device, device_id_type=MESH)
+    has_next(lambda: pl.semaphore_signal(barrier, inc=1, device_id=next_device, device_id_type=MESH))
+    has_prev(lambda: pl.semaphore_signal(barrier, inc=1, device_id=prev_device, device_id_type=MESH))
 
     def predict(k):
         at = pl.ds(k, 1)
@@ -176,7 +177,8 @@
     phi[...] = level[0]
     gz[z] = level[0]
 
-    pl.semaphore_wait(barrier, (LINE - 1) + len(offsets) + 2)
+    ends = lax.div(place + last, last + 1) + lax.div(2 * last - place, last + 1)
+    pl.semaphore_wait(barrier, (LINE - 1) + len(offsets) + ends)
 
     def remote(src, dst, send, recv, device):
         return pltpu.make_async_remote_copy(
@@ -224,7 +226,8 @@
     to_prev = remote(mult.at[pl.ds(0, 8)], from_next, e_send.at[0], e_recv.at[0], prev_device)
     to_next = remote(edge, from_prev, e_send.at[1], e_recv.at[1], next_device)
     z_maps, z_all = gather_maps(0, "tm_2", gz)
-    run([to_prev, to_next])
+    has_prev(to_prev.start)
+    has_next(to_next.start)
     half = count // 2
 
     @pl.when(core == 0)
@@ -256,9 +259,14 @@
 
     for copy in in_copies[8:16]:
         copy.wait()
-    to_prev.wait_recv()
+    has_next(to_prev.wait_recv)
+
+    @pl.when(place == last)
+    def _():
+        from_next[...] = jnp.zeros((8, ns), F32)
+
     following[pl.ds(0, top), :] = mult[pl.ds(1, top), :]
-    following[pl.ds(top, 1), :] = jnp.where(place == last, 0.0, from_next[pl.ds(0, 1), :])
+    following[pl.ds(top, 1), :] = from_next[pl.ds(0, 1), :]
 
     def gradients(k):
         at = pl.ds(k, 1)
@@ -273,15 +281,28 @@
     )
     grad_input[...] = weighted + input_linear[...] - grad_input[...] + bound[...]
 
-    @pl.when(core == 1)
-    def _():
-        run(z_maps[:6])
+    def suffix_step(i):
+        j = half - 1 - i
+        suffix = rst[2 * j + 1]
+        rst[2 * j] = mm(suffix, am[2 * j + 1])
+        rst[2 * j - 1] = mm(suffix, tree[j])
+
+    def suffixes():
+        rst[top - 1] = am[top]
+        rst[top - 2] = tree[half - 1]
+        pl.loop(1, half - 1)(suffix_step)
+        rst[0] = mm(rst[1], am[1])
 
     for copy in in_copies[16:]:
         copy.wait()
-    to_next.wait_recv()
+    has_prev(to_next.wait_recv)
+
+    @pl.when(place == 0)
+    def _():
+        from_prev[...] = jnp.zeros((8, ns), F32)
+
     defect[pl.ds(1, top), :] = states[pl.ds(1, top), :] - predicted[pl.ds(0, top), :] - offset[pl.ds(1, top), :]
-    entered = jnp.where(place == 0, 0.0, from_prev[pl.ds(0, 1), :])
+    entered = from_prev[pl.ds(0, 1), :]
     defect[pl.ds(0, 1), :] = states[pl.ds(0, 1), :] - entered - offset[pl.ds(0, 1), :]
 
     def source(k):
@@ -290,6 +311,11 @@
         weighted_map[k] = mm(gm[k], bm[k])
 
     pl.loop(0, count, unroll=4)(source)
+
+    @pl.when(core == 1)
+    def _():
+        run(z_maps[:6])
+        suffixes()
 
     @pl.when(core == 1)
     def _():
@@ -321,6 +347,20 @@
     c_line, c_all = gather_vectors(0, "tm_2", cz)
     run(c_line)
 
+    def reach(k):
+        both = jnp.concatenate([bm[k], weighted_map[k]], axis=0)
+        w = mm(both, rst[k], 1, 1)
+        rows = pl.ds(pl.multiple_of(k * nu, nu), nu)
+        wst[rows, :] = w[:nu]
+        gwst[rows, :] = w[nu:]
+
+    def reach_all():
+        pl.loop(0, top, unroll=5)(reach)
+        wst[pl.ds(top * nu, nu), :] = bm[top]
+        gwst[pl.ds(top * nu, nu), :] = weighted_map[top]
+
+    pl.when(core == 1)(reach_all)
+
     z_all.wait_recv()
     gx[x] = line_products(gz, sz, pz)
     x_maps, x_all = gather_maps(1, "tm_1", gx)
@@ -336,17 +376,7 @@
 
     run(x_maps[:6])
 
-    rst[top - 1] = am[top]
-    rst[top - 2] = tree[half - 1]
-
-    def suffix_step(i):
-        j = half - 1 - i
-        suffix = rst[2 * j + 1]
-        rst[2 * j] = mm(suffix, am[2 * j + 1])
-        rst[2 * j - 1] = mm(suffix, tree[j])
-
-    pl.loop(1, half - 1)(suffix_step)
-    rst[0] = mm(rst[1], am[1])
+    pl.when(core == 0)(suffixes)
 
     c_all.wait_recv()
     group_costate, totals = line_backward(cz, gz, vloc_z)
@@ -356,16 +386,21 @@
     cx_line, cx_all = gather_vectors(1, "tm_1", cx)
     run(cx_line)
 
-    relay(x_maps, gx, 1, 0)
+    pl.when(core == 0)(lambda: relay(x_maps, gx, 1, 0))
 
     def backward(i, v):
         k = top - i
         after[pl.ds(k, 1), :] = v
         return col_mv(v, am[k]) + sources[pl.ds(k, 1), :]
 
-    v = lax.fori_loop(0, half, backward, jnp.zeros((1, ns), F32))
-    relay(x_maps, gx, 1, 1)
-    lax.fori_loop(half, count, backward, v)
+    v = lax.fori_loop(0, half // 2, backward, jnp.zeros((1, ns), F32))
+    pl.when(core == 0)(lambda: relay(x_maps, gx, 1, 1))
+    lax.fori_loop(half // 2, count, backward, v)
+
+    @pl.when(core == 1)
+    def _():
+        relay(x_maps, gx, 1, 0)
+        relay(x_maps, gx, 1, 1)
 
     def respond(k):
         at = pl.ds(k, 1)
@@ -385,19 +420,11 @@
 
     local_state()
 
-    def reach(k):
-        both = jnp.concatenate([bm[k], weighted_map[k]], axis=0)
-        w = mm(both, rst[k], 1, 1)
-        rows = pl.ds(pl.multiple_of(k * nu, nu), nu)
-        wst[rows, :] = w[:nu]
-        gwst[rows, :] = w[nu:]
-
     def gather_reach():
-        pl.loop(0, top, unroll=5)(reach)
-        wst[pl.ds(top * nu, nu), :] = bm[top]
-        gwst[pl.ds(top * nu, nu), :] = weighted_map[top]
+        pl.when(core == 0)(reach_all)
         mmat[...] = mm(wst[...], gwst[...], 0, 0)
 
+    line_rest(gz, sz, pz)
     cx_all.wait_recv()
 
     x_all.wait_recv()
@@ -432,7 +459,6 @@
     sy[y] = jnp.broadcast_to(totals, (8, ns))
     s_line, s_all = gather_vectors(2, "tm_0", sy)
     run(s_line)
-    line_rest(gz, sz, pz)
     line_rest(gx, sx, px)
     tback[...] = mm(sx[x], sz[z])
     t_zero = col_mv(vloc_x[x, pl.ds(0, 1), :], sz[z]) + vloc_z[z, pl.ds(0, 1), :]
@@ -511,7 +537,10 @@
         state_step[pl.ds(k, 1), :] = correction
         return row_mv(am[k], correction) + pushes[pl.ds(k, 1), :]
 
-    lax.fori_loop(0, count, forward, jnp.zeros((1, ns), F32))
+    def local_steps():
+        lax.fori_loop(0, count, forward, jnp.zeros((1, ns), F32))
+
+    local_steps()
 
     sum_line.wait_recv()
     plane_state = jnp.sum(plane_sum[:, 0:1, :], axis=0)
@@ -540,36 +569,44 @@
     in_group = line_state(lambda p: groups[p], gx, x)
     x_zero = row_mv(pz[z], in_group) + in_line
 
-    for by in range(1, LINE):
-        @pl.when(y >= by)
-        def _(by=by):
-            ahead[by - 1].wait_recv()
-
-    @pl.when(y == 0)
-    def _():
-        entry[...] = jnp.zeros((8, ns), F32)
-
-    def enter(vector):
-        entry[...] = jnp.broadcast_to(vector, (8, ns))
-
     at_plane = lambda p: fy[p, pl.ds(0, 1), :]
 
-    @pl.when(y == 1)
-    def _():
-        enter(at_plane(0))
+    def set_base(vector):
+        avec[...] = jnp.broadcast_to(vector, (8, ns))
+
+    @pl.when(y <= 1)
+    def _():
+        set_base(x_zero)
 
     @pl.when(y == 2)
     def _():
-        enter(row_mv(om1[...], at_plane(0)) + at_plane(1))
+        through = tforw[...]
+        tforw[...] = mm(through, om1[...])
+        ahead[0].wait_recv()
+        set_base(row_mv(through, at_plane(1)) + x_zero)
 
     @pl.when(y == LINE - 1)
     def _():
+        through = tforw[...]
         third.wait_recv()
         for copy in passed:
             copy.wait_recv()
-        enter(row_mv(om2[...], row_mv(om1[...], at_plane(0)) + at_plane(1)) + at_plane(2))
-
-    x_in = row_mv(tforw[...], entry[pl.ds(0, 1), :]) + x_zero
+        tforw[...] = mm(mm(through, om2[...]), om1[...])
+        ahead[0].wait_recv()
+        ahead[1].wait_recv()
+        set_base(row_mv(through, row_mv(om2[...], at_plane(1)) + at_plane(2)) + x_zero)
+
+    @pl.when(y == 0)
+    def _():
+        entry[...] = avec[...]
+
+    for by in range(1, LINE):
+        @pl.when(y == by)
+        def _(by=by):
+            ahead[by - 1].wait_recv()
+            entry[...] = jnp.broadcast_to(row_mv(tforw[...], at_plane(0)), (8, ns)) + avec[...]
+
+    x_in = entry[pl.ds(0, 1), :]
     xc = as_column(x_in)
     out_x, out_m = pl.ds(0, count), pl.ds(count, count)
     packed[pl.ds(0, 1), :] = state_step[pl.ds(0, 1), :] + x_in
@@ -608,7 +645,9 @@
     values = jnp.where(lanes == 0, primal, jnp.where(lanes == 1, dual, complement))
     packed[pl.ds(3 * count, 8), :] = jnp.sqrt(values)
 
-    for copy in [to_prev, to_next, z_all, x_all, c_all, cx_all, s_all, sum_line, own_line]:
+    has_prev(to_prev.wait_send)
+    has_next(to_next.wait_send)
+    for copy in [z_all, x_all, c_all, cx_all, s_all, sum_line, own_line]:
         copy.wait_send()
 
     for by in range(1, LINE):

time: 48.4 us -> 47.7 us (0.986)
  Pallas kernels: 47.5 us -> 46.7 us
    pallas_call x1, Pallas kernels: 46.9 us -> 46.1 us  [local(): pl.pallas_call(kernel, out_shape=pltpu.VMEM((3 * count + 8, ns), F32), in...]
where the time goes in v4:
time: 47.7 us; the launch traced here: 47.3 us
  Pallas kernels  46.7 us (98%)
  between operations  0.65 us (1%)
    pallas_call x1, Pallas kernels, local(): pl.pallas_call(kernel, out_shape=pltpu.VMEM((3 * count + 8, ns), F32), in...  46.1 us

profile of v4, /device:TPU:24, one launch (start us, length us, event | category | flops | bytes accessed | tf_op | source)
XLA Modules:
  0.0 47.3 jit_solution(12836791647062969166)
XLA Ops:
  0.6 46.1 %riccati.1.packed = f32[56,256]{1,0:T(8,128)S(1)} custom-call(f32[16,256,256]{2,1,0:T(8,128)} %state_map_h.1, f32[16,64,256]{2,1,0:T(8,128)} %input_map_h.1, f32[16,256,256]{2,1,0:T(8,128)} %closed_loop_h.1, f32[16,64,256]{2,1,0:T(8,128)} %feedback_h.1, f32[16,256,256]{2,1,0:T(8,128)} %value_h.1, f32[16,64,64]{2,1,0:T(8,128)} %gain_h.1, f32[64,64]{1,0:T(8,128)} %weight_h.1, ...), custom_call_target="tpu_custom_call" | custom-call | tf_op jit(solution)/shard_map/riccati/pallas_call | solution.py:704
  46.7 0.6 %unpack.1 = (f32[16,256]{1,0:T(8,128)}, f32[16,64]{1,0:T(8,128)}, f32[16,256]{1,0:T(8,128)}, f32[16,64]{1,0:T(8,128)}, f32[3]{0:T(128)}) custom-call(f32[56,256]{1,0:T(8,128)S(1)} %riccati.1.packed), custom_call_target="tpu_custom_call" | custom-call | tf_op jit(solution)/shard_map/unpack/pallas_call | solution.py:715

commit v5 on v4

--- a/solution.py
+++ b/solution.py
@@ -234,6 +234,7 @@
     def _():
         run(z_maps[:6])
 
+    qt[0] = identity_matrix(ns)
     qt[1] = jnp.transpose(am[0])
     qt[2] = jnp.transpose(tree[0])
 
@@ -251,11 +252,13 @@
 
     for copy in in_copies[5:8]:
         copy.wait()
-    pl.loop(0, top, unroll=5)(predict)
+    pl.loop(0, 10, unroll=5)(predict)
 
     @pl.when(core == 0)
     def _():
         relay(z_maps, gz, 0, 1)
+
+    pl.loop(10, top, unroll=5)(predict)
 
     for copy in in_copies[8:16]:
         copy.wait()
@@ -569,6 +572,17 @@
     in_group = line_state(lambda p: groups[p], gx, x)
     x_zero = row_mv(pz[z], in_group) + in_line
 
+    s_all.wait_recv()
+    totals = jnp.sum(sy[:, 0:1, :], axis=0)
+    horizon = count * LINE**3
+    pick = lambda n: jnp.sum(jnp.where(lane == n, totals, 0.0), axis=1, keepdims=True)
+    primal = pick(0) / (pick(3) + floor_share * horizon * ns)
+    dual = pick(1) / (pick(4) + floor_share * horizon * (ns + nu))
+    complement = pick(2) / (pick(5) + floor_share * horizon * nu)
+    lanes = lax.broadcasted_iota(jnp.int32, (8, ns), 1)
+    values = jnp.where(lanes == 0, primal, jnp.where(lanes == 1, dual, complement))
+    packed[pl.ds(3 * count, 8), :] = jnp.sqrt(values)
+
     at_plane = lambda p: fy[p, pl.ds(0, 1), :]
 
     def set_base(vector):
@@ -608,18 +622,11 @@
 
     x_in = entry[pl.ds(0, 1), :]
     xc = as_column(x_in)
-    out_x, out_m = pl.ds(0, count), pl.ds(count, count)
-    packed[pl.ds(0, 1), :] = state_step[pl.ds(0, 1), :] + x_in
-
-    def settle(k):
-        at = pl.ds(k, 1)
-        packed[at, :] = state_step[at, :] + col_apply(xc, qt[k])
-
-    pl.loop(1, count, unroll=5)(settle)
 
     def close(k):
         at = pl.ds(k, 1)
-        now = packed[at, :]
+        now = state_step[at, :] + col_apply(xc, qt[k])
+        packed[at, :] = now
         sources[at, :] = row_mv(vm[k], now - defect[at, :])
         input_linear[at, :] = row_mv(fm[k], now)
 
@@ -633,17 +640,6 @@
         step, iw[...], (((1,), (1,)), ((), ())), precision=PRECISE, preferred_element_type=F32
     )
     packed[pl.ds(2 * count, count), pl.ds(HALF, nu)] = chosen * (grad_input[...] + weighted + pulled[...])
-
-    s_all.wait_recv()
-    totals = jnp.sum(sy[:, 0:1, :], axis=0)
-    horizon = count * LINE**3
-    pick = lambda n: jnp.sum(jnp.where(lane == n, totals, 0.0), axis=1, keepdims=True)
-    primal = pick(0) / (pick(3) + floor_share * horizon * ns)
-    dual = pick(1) / (pick(4) + floor_share * horizon * (ns + nu))
-    complement = pick(2) / (pick(5) + floor_share * horizon * nu)
-    lanes = lax.broadcasted_iota(jnp.int32, (8, ns), 1)
-    values = jnp.where(lanes == 0, primal, jnp.where(lanes == 1, dual, complement))
-    packed[pl.ds(3 * count, 8), :] = jnp.sqrt(values)
 
     has_prev(to_prev.wait_send)
     has_next(to_next.wait_send)

time: 47.7 us -> 47.7 us (level)
  no operation moved by 1% of the time
where the time goes in v5:
time: 47.7 us; the launch traced here: 47.2 us
  Pallas kernels  46.5 us (97%)
  between operations  0.65 us (1%)
    pallas_call x1, Pallas kernels, local(): pl.pallas_call(kernel, out_shape=pltpu.VMEM((3 * count + 8, ns), F32), in...  45.9 us

profile of v5, /device:TPU:24, one launch (start us, length us, event | category | flops | bytes accessed | tf_op | source)
XLA Modules:
  0.0 47.2 jit_solution(4558685590356997804)
XLA Ops:
  0.6 45.9 %riccati.1.packed = f32[56,256]{1,0:T(8,128)S(1)} custom-call(f32[16,256,256]{2,1,0:T(8,128)} %state_map_h.1, f32[16,64,256]{2,1,0:T(8,128)} %input_map_h.1, f32[16,256,256]{2,1,0:T(8,128)} %closed_loop_h.1, f32[16,64,256]{2,1,0:T(8,128)} %feedback_h.1, f32[16,256,256]{2,1,0:T(8,128)} %value_h.1, f32[16,64,64]{2,1,0:T(8,128)} %gain_h.1, f32[64,64]{1,0:T(8,128)} %weight_h.1, ...), custom_call_target="tpu_custom_call" | custom-call | tf_op jit(solution)/shard_map/riccati/pallas_call | solution.py:700
  46.5 0.6 %unpack.1 = (f32[16,256]{1,0:T(8,128)}, f32[16,64]{1,0:T(8,128)}, f32[16,256]{1,0:T(8,128)}, f32[16,64]{1,0:T(8,128)}, f32[3]{0:T(128)}) custom-call(f32[56,256]{1,0:T(8,128)S(1)} %riccati.1.packed), custom_call_target="tpu_custom_call" | custom-call | tf_op jit(solution)/shard_map/unpack/pallas_call | solution.py:711
